TPU v7x, 256 devices: a whole 4x4x8 slice. The times are simulated.
256 devices in a mesh: band: 32 (over y_lo, z, core), slab: 8 (over x, y_hi).
Axes of the slice: x: 4, y: 4 (y_hi: 2, y_lo: 2; y = y_hi * 2 + y_lo), z: 8, core: 2. Of those that a mesh axis runs over, the one named last changes fastest.
Arguments:
- orbitals: bfloat16 [64, 128, 4096], P('band', 'slab'), may hold values from -6 to 6
- occupation: bfloat16 [64], P('band'), may hold values from 0.25 to 1
Outputs:
- exchange_field: float32 [64, 128, 4096], P('band', 'slab')
All inputs are finite; a program needn't handle non-finite values.
Results may differ from a plain program's by a relative error of at most 0.001.
Values may be sent and summed in bfloat16 or wider, within the bound.
No kernel may reach another device: no remote copies, remote signals or barrier semaphores. Data moves between devices by JAX's collectives and lax.ppermute only.
A program may use at most 64 MiB of HBM per device.

v0:
```python
import math

import jax
import jax.numpy as jnp
from jax import lax
from jax.sharding import PartitionSpec as P

NZ = 64
STEPS = 3


screening = 0.5
ratio_mid = (12.0 + 2.0 * screening) / 12.0
root_term = math.sqrt(ratio_mid * ratio_mid - 1.0)
decay_ratio = ratio_mid - root_term
coeff_zero = 1.0 / (6.0 * root_term)
coeff_one = -2.0 * decay_ratio * coeff_zero
coeff_two = 2.0 * decay_ratio * decay_ratio * coeff_zero


def with_halo(array, sides, width):
    for axis, dim in sides:
        size, length = (lax.axis_size(axis), array.shape[dim])
        up = [(i, (i + 1) % size) for i in range(size - 1)]
        down = [(j, i) for i, j in up]
        last = lax.slice_in_dim(array, length - width, length, axis=dim)
        leading = lax.slice_in_dim(array, 0, width, axis=dim)
        before = lax.ppermute(last, axis, up)
        after = lax.ppermute(leading, axis, down)
        array = jnp.concatenate([before, array, after], axis=dim)
    return array


def passed_along(array, axis, by):
    size = lax.axis_size(axis)
    return lax.ppermute(array, axis, [(i, (i + by) % size) for i in range(size)])


def cross_sum(values):
    rest = ((0, 0),) * (values.ndim - 1)
    padded_y = jnp.pad(values, rest + ((NZ, NZ),))
    along_y = padded_y[..., 2 * NZ :] + padded_y[..., : -2 * NZ]
    narrow = jnp.pad(values, rest + ((1, 1),))
    column = jnp.arange(values.shape[-1], dtype=jnp.int32) % NZ
    left_side = jnp.where(column != 0, narrow[..., :-2], 0.0)
    right_side = jnp.where(column != NZ - 1, narrow[..., 2:], 0.0)
    return along_y + (left_side + right_side)


def neighbour_planes(extended):
    return extended[:, :, 2:] + extended[:, :, :-2] + cross_sum(extended[:, :, 1:-1])


def per_device(orbitals, occupation):
    planes = orbitals.shape[1]
    own_extended = with_halo(orbitals, (("slab", 1),), 2)
    own_wide = own_extended.astype(jnp.float32)
    running = jnp.zeros(orbitals.shape, jnp.float32)
    visiting = (orbitals, occupation)
    for visit in range(STEPS + 1):
        if visit > 0:
            visiting = passed_along((visiting[0], visiting[1]), "band", 1)
        visitor_orbitals, visitor_weights = visiting
        if visit == 0:
            visitor_wide = own_wide
        else:
            visitor_wide = with_halo(visitor_orbitals, (("slab", 1),), 2).astype(jnp.float32)
        density_wide = own_wide[:, None] * visitor_wide[None]
        first_wide = -neighbour_planes(density_wide) / 6.0
        global_plane = lax.axis_index("slab") * planes + jnp.arange(planes + 2, dtype=jnp.int32) - 1
        inside = (global_plane >= 0) & (global_plane < planes * lax.axis_size("slab"))
        first_wide = jnp.where(inside[:, None], first_wide, 0.0)
        density = density_wide[:, :, 2:-2]
        first_term = first_wide[:, :, 1:-1]
        second_term = -neighbour_planes(first_wide) / 3.0 - density
        potential = coeff_zero * density + coeff_one * first_term + coeff_two * second_term
        visitor = visitor_orbitals.astype(jnp.float32)
        weights = visitor_weights.astype(jnp.float32)
        running = running - jnp.sum(
            weights[None, :, None, None] * visitor[None] * potential, axis=1
        )
    return running


def solution(mesh):
    in_specs = (P("band", "slab", None), P("band"))
    out_specs = P("band", "slab", None)
    return jax.shard_map(
        per_device, mesh=mesh, in_specs=in_specs, out_specs=out_specs, check_vma=False
    )
```

profile of v0, /device:TPU:16, one launch (start us, length us, event | category | flops | bytes accessed | tf_op | source)
XLA Modules:
  0.0 104.0 jit_solution(18176715507416551858)
XLA Ops:
  0.0 1.0 fusion.55
  1.0 3.2 %collective-permute-start = (bf16[2,2,4096]{2,1,0:T(2,128)(2,1)S(1)}, bf16[2,2,4096]{2,1,0:T(2,128)(2,1)S(1)}, u32[]{:S(2)}, u32[]{:S(2)}) collective-permute-start(bf16[2,2,4096]{2,1,0:T(2,128)(2,1)S(1)} %get-tuple-element.17), channel_id=1, source_target_pairs={{0,1},{1,2},{2,3},{3,4},{4,5},{5,6},{6,7},{8,9},{9,10},{10,11},{11... | collective-permute-start | bytes 98312 | tf_op jit(solution)/shard_map/ppermute | solution.py:28
  4.2 4.2 %collective-permute-start.1 = (bf16[2,2,4096]{2,1,0:T(2,128)(2,1)S(1)}, bf16[2,2,4096]{2,1,0:T(2,128)(2,1)S(1)}, u32[]{:S(2)}, u32[]{:S(2)}) collective-permute-start(bf16[2,2,4096]{2,1,0:T(2,128)(2,1)S(1)} %get-tuple-element.18), channel_id=1, source_target_pairs={{1,0},{2,1},{3,2},{4,3},{5,4},{6,5},{7,6},{9,8},{10,9},{11,10},{12... | collective-permute-start | bytes 98312 | tf_op jit(solution)/shard_map/ppermute | solution.py:29
  8.4 1.6 %collective-permute-start.2 = (bf16[2]{0:T(256)(128)(2,1)}, bf16[2]{0:T(256)(128)(2,1)S(1)}, u32[]{:S(2)}, u32[]{:S(2)}) collective-permute-start(bf16[2]{0:T(256)(128)(2,1)} %param.3), channel_id=1, source_target_pairs={{0,8},{8,16},{16,24},{24,32},{32,40},{40,48},{48,56},{56,64},{64,7... | collective-permute-start | bytes 20 | tf_op jit(solution)/shard_map/ppermute | solution.py:36
  10.6 1.9 %convert_multiply_fusion.3 = f32[2,16,4096]{2,1,0:T(8,128)} fusion(bf16[2,16,4096]{2,1,0:T(8,128)(2,1)} %param.2, f32[2]{0:T(128)S(1)} %convert_element_type.76), kind=kLoop, calls=%fused_computation.64 | loop fusion | flops 262144 | bytes 786440 | tf_op jit(solution)/shard_map/mul | solution.py:80
  12.5 2.8 %collective-permute-done.2 = bf16[2]{0:T(256)(128)(2,1)S(1)} collective-permute-done((bf16[2]{0:T(256)(128)(2,1)}, bf16[2]{0:T(256)(128)(2,1)S(1)}, u32[]{:S(2)}, u32[]{:S(2)}) %collective-permute-start.2) | collective-permute-done | bytes 36 | tf_op jit(solution)/shard_map/ppermute | solution.py:36
  15.3 5.1 %collective-permute-done.6 = bf16[2]{0:T(256)(128)(2,1)S(1)} collective-permute-done((bf16[2]{0:T(256)(128)(2,1)S(1)}, bf16[2]{0:T(256)(128)(2,1)S(1)}, u32[]{:S(2)}, u32[]{:S(2)}) %collective-permute-start.6) | collective-permute-done | bytes 36 | tf_op jit(solution)/shard_map/ppermute | solution.py:36
  20.4 5.1 %collective-permute-done.10 = bf16[2]{0:T(256)(128)(2,1)S(1)} collective-permute-done((bf16[2]{0:T(256)(128)(2,1)S(1)}, bf16[2]{0:T(256)(128)(2,1)S(1)}, u32[]{:S(2)}, u32[]{:S(2)}) %collective-permute-start.10) | collective-permute-done | bytes 36 | tf_op jit(solution)/shard_map/ppermute | solution.py:36
  25.5 1.1 %maximum_convert_fusion = f32[2,20,4096]{2,1,0:T(8,128)S(1)} fusion(bf16[2,2,4096]{2,1,0:T(2,128)(2,1)S(1)} %collective-permute-done.1, bf16[2,16,4096]{2,1,0:T(8,128)(2,1)} %param.2, bf16[2,2,4096]{2,1,0:T(2,128)(2,1)S(1)} %collective-permute-done), kind=kLoop, calls=%fused_computation.65 | loop fusion | flops 983040 | bytes 983040 | tf_op jit(solution)/shard_map/convert_element_type | solution.py:57
  26.7 4.4 %collective-permute-start.4 = (bf16[2,2,4096]{2,1,0:T(2,128)(2,1)S(1)}, bf16[2,2,4096]{2,1,0:T(2,128)(2,1)S(1)}, u32[]{:S(2)}, u32[]{:S(2)}) collective-permute-start(bf16[2,2,4096]{2,1,0:T(2,128)(2,1)S(1)} %get-tuple-element.13), channel_id=1, source_target_pairs={{0,1},{1,2},{2,3},{3,4},{4,5},{5,6},{6,7},{8,9},{9,10},{10,11},{11... | collective-permute-start | bytes 98312 | tf_op jit(solution)/shard_map/ppermute | solution.py:28
  31.1 3.0 %collective-permute-start.5 = (bf16[2,2,4096]{2,1,0:T(2,128)(2,1)S(1)}, bf16[2,2,4096]{2,1,0:T(2,128)(2,1)S(1)}, u32[]{:S(2)}, u32[]{:S(2)}) collective-permute-start(bf16[2,2,4096]{2,1,0:T(2,128)(2,1)S(1)} %get-tuple-element.14), channel_id=1, source_target_pairs={{1,0},{2,1},{3,2},{4,3},{5,4},{6,5},{7,6},{9,8},{10,9},{11,10},{12... | collective-permute-start | bytes 98312 | tf_op jit(solution)/shard_map/ppermute | solution.py:29
  34.2 0.9 convert_multiply_fusion.2
  35.1 4.6 %collective-permute-done.5 = bf16[2,2,4096]{2,1,0:T(2,128)(2,1)S(1)} collective-permute-done((bf16[2,2,4096]{2,1,0:T(2,128)(2,1)S(1)}, bf16[2,2,4096]{2,1,0:T(2,128)(2,1)S(1)}, u32[]{:S(2)}, u32[]{:S(2)}) %collective-permute-start.5) | collective-permute-done | bytes 32800 | tf_op jit(solution)/shard_map/ppermute | solution.py:29
  39.8 2.3 %collective-permute-done.7 = bf16[2,16,4096]{2,1,0:T(8,128)(2,1)S(1)} collective-permute-done((bf16[2,16,4096]{2,1,0:T(8,128)(2,1)S(1)}, bf16[2,16,4096]{2,1,0:T(8,128)(2,1)S(1)}, u32[]{:S(2)}, u32[]{:S(2)}) %collective-permute-start.7) | collective-permute-done | bytes 262176 | tf_op jit(solution)/shard_map/ppermute | solution.py:36
  42.1 5.4 %collective-permute-start.8 = (bf16[2,2,4096]{2,1,0:T(2,128)(2,1)S(1)}, bf16[2,2,4096]{2,1,0:T(2,128)(2,1)S(1)}, u32[]{:S(2)}, u32[]{:S(2)}) collective-permute-start(bf16[2,2,4096]{2,1,0:T(2,128)(2,1)S(1)} %get-tuple-element.19), channel_id=1, source_target_pairs={{0,1},{1,2},{2,3},{3,4},{4,5},{5,6},{6,7},{8,9},{9,10},{10,11},{11... | collective-permute-start | bytes 98312 | tf_op jit(solution)/shard_map/ppermute | solution.py:28
  47.5 2.0 %collective-permute-start.9 = (bf16[2,2,4096]{2,1,0:T(2,128)(2,1)S(1)}, bf16[2,2,4096]{2,1,0:T(2,128)(2,1)S(1)}, u32[]{:S(2)}, u32[]{:S(2)}) collective-permute-start(bf16[2,2,4096]{2,1,0:T(2,128)(2,1)S(1)} %get-tuple-element.20), channel_id=1, source_target_pairs={{1,0},{2,1},{3,2},{4,3},{5,4},{6,5},{7,6},{9,8},{10,9},{11,10},{12... | collective-permute-start | bytes 98312 | tf_op jit(solution)/shard_map/ppermute | solution.py:29
  49.6 0.9 convert_multiply_fusion.1
  50.5 5.2 %collective-permute-done.9 = bf16[2,2,4096]{2,1,0:T(2,128)(2,1)S(1)} collective-permute-done((bf16[2,2,4096]{2,1,0:T(2,128)(2,1)S(1)}, bf16[2,2,4096]{2,1,0:T(2,128)(2,1)S(1)}, u32[]{:S(2)}, u32[]{:S(2)}) %collective-permute-start.9) | collective-permute-done | bytes 32800 | tf_op jit(solution)/shard_map/ppermute | solution.py:29
  55.8 1.6 %collective-permute-done.11 = bf16[2,16,4096]{2,1,0:T(8,128)(2,1)S(1)} collective-permute-done((bf16[2,16,4096]{2,1,0:T(8,128)(2,1)S(1)}, bf16[2,16,4096]{2,1,0:T(8,128)(2,1)S(1)}, u32[]{:S(2)}, u32[]{:S(2)}) %collective-permute-start.11) | collective-permute-done | bytes 262176 | tf_op jit(solution)/shard_map/ppermute | solution.py:36
  57.5 6.3 %collective-permute-start.12 = (bf16[2,2,4096]{2,1,0:T(2,128)(2,1)S(1)}, bf16[2,2,4096]{2,1,0:T(2,128)(2,1)S(1)}, u32[]{:S(2)}, u32[]{:S(2)}) collective-permute-start(bf16[2,2,4096]{2,1,0:T(2,128)(2,1)S(1)} %get-tuple-element.15), channel_id=1, source_target_pairs={{0,1},{1,2},{2,3},{3,4},{4,5},{5,6},{6,7},{8,9},{9,10},{10,11},{11... | collective-permute-start | bytes 98312 | tf_op jit(solution)/shard_map/ppermute | solution.py:28
  63.9 2.1 %collective-permute-start.13 = (bf16[2,2,4096]{2,1,0:T(2,128)(2,1)S(1)}, bf16[2,2,4096]{2,1,0:T(2,128)(2,1)S(1)}, u32[]{:S(2)}, u32[]{:S(2)}) collective-permute-start(bf16[2,2,4096]{2,1,0:T(2,128)(2,1)S(1)} %get-tuple-element.16), channel_id=1, source_target_pairs={{1,0},{2,1},{3,2},{4,3},{5,4},{6,5},{7,6},{9,8},{10,9},{11,10},{12... | collective-permute-start | bytes 98312 | tf_op jit(solution)/shard_map/ppermute | solution.py:29
  66.0 0.9 convert_multiply_fusion
  66.9 5.2 %collective-permute-done.13 = bf16[2,2,4096]{2,1,0:T(2,128)(2,1)S(1)} collective-permute-done((bf16[2,2,4096]{2,1,0:T(2,128)(2,1)S(1)}, bf16[2,2,4096]{2,1,0:T(2,128)(2,1)S(1)}, u32[]{:S(2)}, u32[]{:S(2)}) %collective-permute-start.13) | collective-permute-done | bytes 32800 | tf_op jit(solution)/shard_map/ppermute | solution.py:29
  73.0 1.3 %slice.279 = f32[2,2,18,4096]{3,2,1,0:T(8,128)} slice(f32[2,2,20,4096]{3,2,1,0:T(8,128)S(1)} %get-tuple-element.12), slice={[0:2], [0:2], [1:19], [0:4096]} | slice | bytes 2359296 | tf_op jit(solution)/shard_map/slice | solution.py:51
  74.3 1.3 %slice.288 = f32[2,2,18,4096]{3,2,1,0:T(8,128)} slice(f32[2,2,20,4096]{3,2,1,0:T(8,128)S(1)} %get-tuple-element.9), slice={[0:2], [0:2], [1:19], [0:4096]} | slice | bytes 2359296 | tf_op jit(solution)/shard_map/slice | solution.py:51
  75.6 1.3 %slice.297 = f32[2,2,18,4096]{3,2,1,0:T(8,128)} slice(f32[2,2,20,4096]{3,2,1,0:T(8,128)S(1)} %get-tuple-element.10), slice={[0:2], [0:2], [1:19], [0:4096]} | slice | bytes 2359296 | tf_op jit(solution)/shard_map/slice | solution.py:51
  76.9 1.4 %slice.306 = f32[2,2,18,4096]{3,2,1,0:T(8,128)} slice(f32[2,2,20,4096]{3,2,1,0:T(8,128)S(1)} %get-tuple-element.11), slice={[0:2], [0:2], [1:19], [0:4096]} | slice | bytes 2359296 | tf_op jit(solution)/shard_map/slice | solution.py:51
  78.2 16.7 %fusion.11 = (f32[2,2,18,4096]{3,2,1,0:T(8,128)S(1)}, f32[2,2,18,4096]{3,2,1,0:T(8,128)S(1)}, f32[2,2,18,4096]{3,2,1,0:T(8,128)S(1)}, f32[2,2,18,4096]{3,2,1,0:T(8,128)}) fusion(f32[2,2,20,4096]{3,2,1,0:T(8,128)S(1)} %get-tuple-element.9, f32[2,2,18,4096]{3,2,1,0:T(8,128)} %slice.288, pred[18]{0:T(512)(128)(4,1)S(1)} %compare_and_fusion, ...), kind=kLoop, calls=%fused_computation.14 | loop fusion | flops 11796480 | bytes 18882578 | tf_op jit(solution)/shard_map/jit(_where)/select_n | solution.py:72
  95.0 1.5 %slice.280 = f32[2,2,16,4096]{3,2,1,0:T(8,128)S(1)} slice(f32[2,2,18,4096]{3,2,1,0:T(8,128)} %get-tuple-element.24), slice={[0:2], [0:2], [1:17], [0:4096]} | slice | bytes 2097152 | tf_op jit(solution)/shard_map/slice | solution.py:74
  98.3 2.4 %fusion.47 = (f32[2,16,4096]{2,1,0:T(8,128)S(1)}, f32[2,16,4096]{2,1,0:T(8,128)S(1)}) fusion(f32[2,2,18,4096]{3,2,1,0:T(8,128)S(1)} %copy-done, f32[2,2,16,4096]{3,2,1,0:T(8,128)S(1)} %slice.280, f32[2,2,20,4096]{3,2,1,0:T(8,128)S(1)} %get-tuple-element.12, f32[2,16,4096]{2,1,0:T(8,128)S(1)} %copy-done.1, pred[4096]{0:T(1024)(128)(4,1)S(1)} %get-tuple-element.25, ...), kind=kLoop, calls=%fused_computation.55 | loop fusion | flops 8650752 | bytes 10493952 | tf_op jit(solution)/shard_map/reduce_sum | solution.py:79
  100.7 2.4 %fusion.31 = (f32[2,16,4096]{2,1,0:T(8,128)S(1)}, f32[2,16,4096]{2,1,0:T(8,128)S(1)}) fusion(f32[2,2,18,4096]{3,2,1,0:T(8,128)S(1)} %get-tuple-element.22, f32[2,2,16,4096]{3,2,1,0:T(8,128)S(1)} %slice.298, f32[2,2,20,4096]{3,2,1,0:T(8,128)S(1)} %get-tuple-element.10, f32[2,16,4096]{2,1,0:T(8,128)S(1)} %copy-done.3, ...), kind=kLoop, calls=%fused_computation.37 | loop fusion | flops 8650752 | bytes 10493952 | tf_op jit(solution)/shard_map/reduce_sum | solution.py:79
  103.1 0.9 subtract_subtract_fusion
  (37 shorter events, 4.0 us)
Async XLA Ops:
  0.0 26.6 %collective-permute-start.3 = (bf16[2,16,4096]{2,1,0:T(8,128)(2,1)}, bf16[2,16,4096]{2,1,0:T(8,128)(2,1)S(1)}, u32[]{:S(2)}, u32[]{:S(2)}) collective-permute-start(bf16[2,16,4096]{2,1,0:T(8,128)(2,1)} %param.2), channel_id=1, source_target_pairs={{0,8},{8,16},{16,24},{24,32},{32,40},{40,48},{48,56},{56,64},{64,7... | collective-permute-start | bytes 786440 | tf_op jit(solution)/shard_map/ppermute | solution.py:36
  1.0 24.5 %collective-permute-start = (bf16[2,2,4096]{2,1,0:T(2,128)(2,1)S(1)}, bf16[2,2,4096]{2,1,0:T(2,128)(2,1)S(1)}, u32[]{:S(2)}, u32[]{:S(2)}) collective-permute-start(bf16[2,2,4096]{2,1,0:T(2,128)(2,1)S(1)} %get-tuple-element.17), channel_id=1, source_target_pairs={{0,1},{1,2},{2,3},{3,4},{4,5},{5,6},{6,7},{8,9},{9,10},{10,11},{11... | collective-permute-start | bytes 98312 | tf_op jit(solution)/shard_map/ppermute | solution.py:28
  4.2 21.3 %collective-permute-start.1 = (bf16[2,2,4096]{2,1,0:T(2,128)(2,1)S(1)}, bf16[2,2,4096]{2,1,0:T(2,128)(2,1)S(1)}, u32[]{:S(2)}, u32[]{:S(2)}) collective-permute-start(bf16[2,2,4096]{2,1,0:T(2,128)(2,1)S(1)} %get-tuple-element.18), channel_id=1, source_target_pairs={{1,0},{2,1},{3,2},{4,3},{5,4},{6,5},{7,6},{9,8},{10,9},{11,10},{12... | collective-permute-start | bytes 98312 | tf_op jit(solution)/shard_map/ppermute | solution.py:29
  8.4 6.9 %collective-permute-start.2 = (bf16[2]{0:T(256)(128)(2,1)}, bf16[2]{0:T(256)(128)(2,1)S(1)}, u32[]{:S(2)}, u32[]{:S(2)}) collective-permute-start(bf16[2]{0:T(256)(128)(2,1)} %param.3), channel_id=1, source_target_pairs={{0,8},{8,16},{16,24},{24,32},{32,40},{40,48},{48,56},{56,64},{64,7... | collective-permute-start | bytes 20 | tf_op jit(solution)/shard_map/ppermute | solution.py:36
  15.3 5.1 %collective-permute-start.6 = (bf16[2]{0:T(256)(128)(2,1)S(1)}, bf16[2]{0:T(256)(128)(2,1)S(1)}, u32[]{:S(2)}, u32[]{:S(2)}) collective-permute-start(bf16[2]{0:T(256)(128)(2,1)S(1)} %collective-permute-done.2), channel_id=1, source_target_pairs={{0,8},{8,16},{16,24},{24,32},{32,40},{40,48},{48,56},{56,64},{64,7... | collective-permute-start | bytes 20 | tf_op jit(solution)/shard_map/ppermute | solution.py:36
  20.4 5.1 %collective-permute-start.10 = (bf16[2]{0:T(256)(128)(2,1)S(1)}, bf16[2]{0:T(256)(128)(2,1)S(1)}, u32[]{:S(2)}, u32[]{:S(2)}) collective-permute-start(bf16[2]{0:T(256)(128)(2,1)S(1)} %collective-permute-done.6), channel_id=1, source_target_pairs={{0,8},{8,16},{16,24},{24,32},{32,40},{40,48},{48,56},{56,64},{64,7... | collective-permute-start | bytes 20 | tf_op jit(solution)/shard_map/ppermute | solution.py:36
  26.7 8.4 %collective-permute-start.4 = (bf16[2,2,4096]{2,1,0:T(2,128)(2,1)S(1)}, bf16[2,2,4096]{2,1,0:T(2,128)(2,1)S(1)}, u32[]{:S(2)}, u32[]{:S(2)}) collective-permute-start(bf16[2,2,4096]{2,1,0:T(2,128)(2,1)S(1)} %get-tuple-element.13), channel_id=1, source_target_pairs={{0,1},{1,2},{2,3},{3,4},{4,5},{5,6},{6,7},{8,9},{9,10},{10,11},{11... | collective-permute-start | bytes 98312 | tf_op jit(solution)/shard_map/ppermute | solution.py:28
  31.1 8.6 %collective-permute-start.5 = (bf16[2,2,4096]{2,1,0:T(2,128)(2,1)S(1)}, bf16[2,2,4096]{2,1,0:T(2,128)(2,1)S(1)}, u32[]{:S(2)}, u32[]{:S(2)}) collective-permute-start(bf16[2,2,4096]{2,1,0:T(2,128)(2,1)S(1)} %get-tuple-element.14), channel_id=1, source_target_pairs={{1,0},{2,1},{3,2},{4,3},{5,4},{6,5},{7,6},{9,8},{10,9},{11,10},{12... | collective-permute-start | bytes 98312 | tf_op jit(solution)/shard_map/ppermute | solution.py:29
  34.1 8.0 %collective-permute-start.7 = (bf16[2,16,4096]{2,1,0:T(8,128)(2,1)S(1)}, bf16[2,16,4096]{2,1,0:T(8,128)(2,1)S(1)}, u32[]{:S(2)}, u32[]{:S(2)}) collective-permute-start(bf16[2,16,4096]{2,1,0:T(8,128)(2,1)S(1)} %collective-permute-done.3), channel_id=1, source_target_pairs={{0,8},{8,16},{16,24},{24,32},{32,40},{40,48},{48,56},{56,64},{64,7... | collective-permute-start | bytes 786440 | tf_op jit(solution)/shard_map/ppermute | solution.py:36
  42.1 8.4 %collective-permute-start.8 = (bf16[2,2,4096]{2,1,0:T(2,128)(2,1)S(1)}, bf16[2,2,4096]{2,1,0:T(2,128)(2,1)S(1)}, u32[]{:S(2)}, u32[]{:S(2)}) collective-permute-start(bf16[2,2,4096]{2,1,0:T(2,128)(2,1)S(1)} %get-tuple-element.19), channel_id=1, source_target_pairs={{0,1},{1,2},{2,3},{3,4},{4,5},{5,6},{6,7},{8,9},{9,10},{10,11},{11... | collective-permute-start | bytes 98312 | tf_op jit(solution)/shard_map/ppermute | solution.py:28
  47.5 8.2 %collective-permute-start.9 = (bf16[2,2,4096]{2,1,0:T(2,128)(2,1)S(1)}, bf16[2,2,4096]{2,1,0:T(2,128)(2,1)S(1)}, u32[]{:S(2)}, u32[]{:S(2)}) collective-permute-start(bf16[2,2,4096]{2,1,0:T(2,128)(2,1)S(1)} %get-tuple-element.20), channel_id=1, source_target_pairs={{1,0},{2,1},{3,2},{4,3},{5,4},{6,5},{7,6},{9,8},{10,9},{11,10},{12... | collective-permute-start | bytes 98312 | tf_op jit(solution)/shard_map/ppermute | solution.py:29
  49.5 8.0 %collective-permute-start.11 = (bf16[2,16,4096]{2,1,0:T(8,128)(2,1)S(1)}, bf16[2,16,4096]{2,1,0:T(8,128)(2,1)S(1)}, u32[]{:S(2)}, u32[]{:S(2)}) collective-permute-start(bf16[2,16,4096]{2,1,0:T(8,128)(2,1)S(1)} %collective-permute-done.7), channel_id=1, source_target_pairs={{0,8},{8,16},{16,24},{24,32},{32,40},{40,48},{48,56},{56,64},{64,7... | collective-permute-start | bytes 786440 | tf_op jit(solution)/shard_map/ppermute | solution.py:36
  57.5 9.4 %collective-permute-start.12 = (bf16[2,2,4096]{2,1,0:T(2,128)(2,1)S(1)}, bf16[2,2,4096]{2,1,0:T(2,128)(2,1)S(1)}, u32[]{:S(2)}, u32[]{:S(2)}) collective-permute-start(bf16[2,2,4096]{2,1,0:T(2,128)(2,1)S(1)} %get-tuple-element.15), channel_id=1, source_target_pairs={{0,1},{1,2},{2,3},{3,4},{4,5},{5,6},{6,7},{8,9},{9,10},{10,11},{11... | collective-permute-start | bytes 98312 | tf_op jit(solution)/shard_map/ppermute | solution.py:28
  63.9 8.2 %collective-permute-start.13 = (bf16[2,2,4096]{2,1,0:T(2,128)(2,1)S(1)}, bf16[2,2,4096]{2,1,0:T(2,128)(2,1)S(1)}, u32[]{:S(2)}, u32[]{:S(2)}) collective-permute-start(bf16[2,2,4096]{2,1,0:T(2,128)(2,1)S(1)} %get-tuple-element.16), channel_id=1, source_target_pairs={{1,0},{2,1},{3,2},{4,3},{5,4},{6,5},{7,6},{9,8},{10,9},{11,10},{12... | collective-permute-start | bytes 98312 | tf_op jit(solution)/shard_map/ppermute | solution.py:29
  96.6 1.0 %copy-start.2 = (f32[2,16,4096]{2,1,0:T(8,128)S(1)}, f32[2,16,4096]{2,1,0:T(8,128)}, u32[]{:S(2)}) copy-start(f32[2,16,4096]{2,1,0:T(8,128)} %convert_multiply_fusion.2) | copy-start | bytes 1572868
  96.7 1.5 %copy-start = (f32[2,2,18,4096]{3,2,1,0:T(8,128)S(1)}, f32[2,2,18,4096]{3,2,1,0:T(8,128)}, u32[]{:S(2)}) copy-start(f32[2,2,18,4096]{3,2,1,0:T(8,128)} %get-tuple-element.24) | copy-start | bytes 3538948
  96.7 1.6 %copy-start.1 = (f32[2,16,4096]{2,1,0:T(8,128)S(1)}, f32[2,16,4096]{2,1,0:T(8,128)}, u32[]{:S(2)}) copy-start(f32[2,16,4096]{2,1,0:T(8,128)} %convert_multiply_fusion.3) | copy-start | bytes 1572868
  98.3 2.4 %copy-start.3 = (f32[2,16,4096]{2,1,0:T(8,128)S(1)}, f32[2,16,4096]{2,1,0:T(8,128)}, u32[]{:S(2)}) copy-start(f32[2,16,4096]{2,1,0:T(8,128)} %convert_multiply_fusion.1) | copy-start | bytes 1572868
  98.3 2.4 %copy-start.4 = (f32[2,16,4096]{2,1,0:T(8,128)S(1)}, f32[2,16,4096]{2,1,0:T(8,128)}, u32[]{:S(2)}) copy-start(f32[2,16,4096]{2,1,0:T(8,128)} %convert_multiply_fusion) | copy-start | bytes 1572868
where the time goes:
time: 104 us
  starting transfers between devices  32.2 us (31%)
  waiting for transfers between devices  31.8 us (31%)
  other arithmetic  30 us (29%)
  local copies, waits for them, and re-layouts  9.71 us (9%)
    ppermute x4, starting transfers between devices, with_halo(): before = lax.ppermute(last, axis, up)  19.2 us
    ppermute x6, waiting for transfers between devices, passed_along(): lax.ppermute(array, axis, [(i, (i + by) % size) for i in range(size)])  16.9 us
    select_n x1, other arithmetic, per_device(): first_wide = jnp.where(inside[:, None], first_wide, 0.0)  16.7 us
    ppermute x4, waiting for transfers between devices, with_halo(): after = lax.ppermute(leading, axis, down)  15 us
    ppermute x4, starting transfers between devices, with_halo(): after = lax.ppermute(leading, axis, down)  11.2 us
    slice x4, local copies, waits for them, and re-layouts, neighbour_planes(): extended[:, :, 1:-1]  5.27 us
    reduce_sum x2, other arithmetic, per_device(): jnp.sum(weights[None, :, None, None] * visitor[None] * potential, axis=1)  4.81 us
    mul x4, other arithmetic, per_device(): weights[None, :, None, None] * visitor[None] * potential  4.66 us
  transfers between devices with their start and end apart: 14, of which 8 were waited for; matrix products, arithmetic and copies ran while one was open for 7% of the time, Pallas kernels for 0%

commit v1 on v0

v1 whole, which is shorter than its diff:
```python
import math

import jax
import jax.numpy as jnp
from jax import lax
from jax.experimental import pallas as pl
from jax.experimental.pallas import tpu as pltpu
from jax.sharding import PartitionSpec as P

NZ = 64
STEPS = 3
LANES = 128
UNROLL = 4

screening = 0.5
ratio_mid = (12.0 + 2.0 * screening) / 12.0
root_term = math.sqrt(ratio_mid * ratio_mid - 1.0)
decay_ratio = ratio_mid - root_term
coeff_zero = 1.0 / (6.0 * root_term)
coeff_one = -2.0 * decay_ratio * coeff_zero
coeff_two = 2.0 * decay_ratio * decay_ratio * coeff_zero

lead = coeff_two / 18.0
slope = (-coeff_one / 6.0) / lead
base = (coeff_zero - coeff_two) / lead

PAIRS = ((0, 0), (1, 1), (0, 1), (1, 0))


def visit_kernel(own_ref, own_halo_ref, visitor_ref, halo_ref, *rest):
    running_ref = rest[0] if len(rest) == 6 else None
    out_ref, rho, rho_y, mid, mid_y = rest[-5:]
    groups = own_ref.shape[2] // LANES
    shape = (8, LANES)
    lane = lax.broadcasted_iota(jnp.int32, shape, 1)
    row = lax.broadcasted_iota(jnp.int32, shape, 0)
    low = lane < NZ
    has_left = lane % NZ != 0
    has_right = lane % NZ != NZ - 1
    zero = jnp.zeros(shape, jnp.float32)

    def lanes_by(v, k):
        return pltpu.roll(v, k % LANES, axis=1)

    def rows_by(v, k):
        return pltpu.roll(v, k % 8, axis=0)

    own_tail = own_halo_ref[:, groups * LANES :].astype(jnp.float32)
    tail = halo_ref[:, groups * LANES :].astype(jnp.float32)
    inside = own_tail > 0.0
    weight = []
    for j in range(2):
        w = jnp.maximum(tail[2 * j : 2 * j + 1], tail[4 + 2 * j : 5 + 2 * j])
        weight.append(jnp.broadcast_to(w * -lead, shape))

    def columns(g):
        return pl.ds(pl.multiple_of(g * LANES, LANES), LANES)

    def both(ref, i, g):
        v = ref[i, :, columns(g)].astype(jnp.float32)
        return v[:8], v[8:]

    for k in range(10):
        rho_y[0, k] = zero
        rho_y[groups + 1, k] = zero
    for k in range(8):
        mid_y[0, k] = zero
        mid_y[groups + 1, k] = zero

    def transverse(v, about_y, at, k):
        left = jnp.where(has_left, lanes_by(v, 1), 0.0)
        right = jnp.where(has_right, lanes_by(v, -1), 0.0)
        across = jnp.where(low, about_y[at - 1, k], about_y[at + 1, k])
        return (about_y[at, k] + across) + (left + right)

    def along(v0, v1, edge_down, edge_up):
        a0, a1 = rows_by(v0, 1), rows_by(v1, 1)
        b0, b1 = rows_by(v0, -1), rows_by(v1, -1)
        first, last = row == 0, row == 7
        n0 = jnp.where(first, edge_down, a0) + jnp.where(last, b1, b0)
        n1 = jnp.where(first, a0, a1) + jnp.where(last, edge_up, b1)
        return n0, n1, a0, b1

    def step_rho(g):
        own = [both(own_ref, i, g) for i in range(2)]
        vis = [both(visitor_ref, j, g) for j in range(2)]
        oh = own_halo_ref[:, columns(g)].astype(jnp.float32)
        vh = halo_ref[:, columns(g)].astype(jnp.float32)
        swapped = jnp.where(row % 4 < 2, rows_by(vh, -2), rows_by(vh, 2))
        vals = []
        for i, j in PAIRS:
            vals += [own[i][0] * vis[j][0], own[i][1] * vis[j][1]]
        vals += [oh * vh, oh * swapped]
        for k, v in enumerate(vals):
            rho[g, k] = v
            rho_y[g + 1, k] = lanes_by(v, NZ)

    def step_mid(g):
        for half in range(2):
            h = rho[g, 8 + half]
            up1, dn1 = rows_by(h, 1), rows_by(h, -1)
            up3, dn3 = rows_by(h, 3), rows_by(h, -3)
            pa, pb = 4 * half, 4 * half + 2
            va0, va1 = rho[g, pa], rho[g, pa + 1]
            vb0, vb1 = rho[g, pb], rho[g, pb + 1]
            na0, na1, first_a, _ = along(va0, va1, dn1, up3)
            nb0, nb1, _, last_b = along(vb0, vb1, dn3, up1)
            body = jnp.where(row == 1, first_a, jnp.where(row == 3, rows_by(vb0, 3), jnp.where(row == 4, rows_by(va1, -3), last_b)))
            nh = jnp.where(row < 4, up1, dn1) + body
            for k, v, n in ((pa, va0, na0), (pa + 1, va1, na1), (pb, vb0, nb0), (pb + 1, vb1, nb1)):
                m = v * slope + (n + transverse(v, rho_y, g + 1, k))
                mid[g, k] = m
                mid_y[g + 1, k] = lanes_by(m, NZ)
            m = h * slope + (nh + transverse(h, rho_y, g + 1, 8 + half))
            mid[g, 8 + half] = jnp.where(inside, m, 0.0)

    def step_out(g):
        vis = [both(visitor_ref, j, g) for j in range(2)]
        scaled = [(weight[j] * vis[j][0], weight[j] * vis[j][1]) for j in range(2)]
        total = [[None, None], [None, None]]
        for half in range(2):
            h = mid[g, 8 + half]
            up1, dn1 = rows_by(h, 1), rows_by(h, -1)
            up3, dn3 = rows_by(h, 3), rows_by(h, -3)
            for at, down, up in ((2 * half, dn1, up3), (2 * half + 1, dn3, up1)):
                i, j = PAIRS[at]
                v = (mid[g, 2 * at], mid[g, 2 * at + 1])
                n = along(*v, down, up)[:2]
                for e in range(2):
                    k = 2 * at + e
                    pot = rho[g, k] * base + (n[e] + transverse(v[e], mid_y, g + 1, k))
                    term = scaled[j][e] * pot
                    total[i][e] = term if total[i][e] is None else total[i][e] + term
        for i in range(2):
            for e in range(2):
                t = total[i][e]
                if running_ref is not None:
                    t = t + running_ref[i, 8 * e : 8 * e + 8, columns(g)]
                out_ref[i, 8 * e : 8 * e + 8, columns(g)] = t

    def sweep(step):
        def body(n, carry):
            for k in range(UNROLL):
                step(n * UNROLL + k)
            return carry

        lax.fori_loop(0, groups // UNROLL, body, 0)

    sweep(step_rho)
    sweep(step_mid)
    sweep(step_out)


def visit(own, own_halo, visitor, halo, running):
    groups = own.shape[2] // LANES
    operands = [own, own_halo, visitor, halo] + ([] if running is None else [running])
    vmem = pl.BlockSpec(memory_space=pltpu.VMEM)
    return pl.pallas_call(
        visit_kernel,
        out_shape=jax.ShapeDtypeStruct(own.shape, jnp.float32),
        in_specs=[vmem] * len(operands),
        out_specs=vmem,
        scratch_shapes=[
            pltpu.VMEM((groups, 10, 8, LANES), jnp.float32),
            pltpu.VMEM((groups + 2, 10, 8, LANES), jnp.float32),
            pltpu.VMEM((groups, 10, 8, LANES), jnp.float32),
            pltpu.VMEM((groups + 2, 8, 8, LANES), jnp.float32),
        ],
        input_output_aliases={} if running is None else {4: 0},
        name="visit",
    )(*operands)


def shifted(array, by):
    size = lax.axis_size("band")
    return lax.ppermute(array, "band", [(i, (i + by) % size) for i in range(size)])


def per_device(orbitals, occupation):
    size = lax.axis_size("slab")
    up = [(i, i + 1) for i in range(size - 1)]
    down = [(j, i) for i, j in up]
    planes = orbitals.shape[1]
    bodies = [orbitals, shifted(orbitals, 1), shifted(orbitals, 2)]
    bodies.append(shifted(bodies[2], 1))
    tail = jnp.broadcast_to(occupation[:, None, None], (2, 2, LANES))

    def edge(at):
        planes_at = lax.slice_in_dim(orbitals, at, at + 2, axis=1)
        return jnp.concatenate([planes_at, tail], axis=2).reshape(4, -1)

    before = lax.ppermute(edge(planes - 2), "slab", up)
    after = lax.ppermute(edge(0), "slab", down)
    halo = jnp.concatenate([before, after], axis=0)
    halos = [halo] + [shifted(halo, s) for s in range(1, STEPS + 1)]
    running = None
    for s in range(STEPS + 1):
        running = visit(orbitals, halo, bodies[s], halos[s], running)
    return running


def solution(mesh):
    return jax.shard_map(
        per_device,
        mesh=mesh,
        in_specs=(P("band", "slab", None), P("band")),
        out_specs=P("band", "slab", None),
        check_vma=False,
    )
```

time: 104 us -> 52.1 us (0.50)
  the two profiles are of different devices: /device:TPU:16 before, /device:TPU:1 now
where the time goes in v1:
time: 52.1 us; the launch traced here: 51.9 us
  Pallas kernels  24.6 us (47%)
  starting transfers between devices  19.1 us (37%)
  local copies, waits for them, and re-layouts  5.11 us (10%)
  waiting for transfers between devices  2.85 us (5%)
    pallas_call x4, Pallas kernels, visit(): pl.pallas_call(visit_kernel, out_shape=jax.ShapeDtypeStruct(own.shape, jn...  24.6 us
    ppermute x6, starting transfers between devices, shifted(): lax.ppermute(array, 'band', [(i, (i + by) % size) for i in range(size)])  13 us
    ppermute x1, starting transfers between devices, per_device(): before = lax.ppermute(edge(planes - 2), 'slab', up)  4.82 us
    unnamed x16, local copies, waits for them, and re-layouts  3.23 us
    ppermute x1, waiting for transfers between devices, per_device(): after = lax.ppermute(edge(0), 'slab', down)  2.51 us
    ppermute x1, starting transfers between devices, per_device(): after = lax.ppermute(edge(0), 'slab', down)  1.29 us
  transfers between devices with their start and end apart: 8, of which 2 were waited for; matrix products, arithmetic and copies ran while one was open for 4% of the time, Pallas kernels for 35%

profile of v1, /device:TPU:1, one launch (start us, length us, event | category | flops | bytes accessed | tf_op | source)
XLA Modules:
  0.0 51.9 jit_solution(6905637392601161344)
XLA Ops:
  0.0 2.5 %collective-permute-start.2 = (bf16[2,16,4096]{2,1,0:T(8,128)(2,1)}, bf16[2,16,4096]{2,1,0:T(8,128)(2,1)S(1)}, u32[]{:S(2)}, u32[]{:S(2)}) collective-permute-start(bf16[2,16,4096]{2,1,0:T(8,128)(2,1)} %own_ref.7), channel_id=1, source_target_pairs={{0,16},{8,24},{16,32},{24,40},{32,48},{40,56},{48,64},{56,72},{64,... | collective-permute-start | bytes 786440 | tf_op jit(solution)/shard_map/ppermute | solution.py:176
  2.5 1.0 %fusion = (bf16[2,2,4096]{2,1,0:T(2,128)(2,1)S(1)}, bf16[2,2,4096]{2,1,0:T(2,128)(2,1)S(1)}) fusion(bf16[2,16,4096]{2,1,0:T(8,128)(2,1)} %own_ref.7), kind=kLoop, calls=%fused_computation.3 | loop fusion | bytes 131072 | tf_op jit(solution)/shard_map/slice | solution.py:189
  3.5 0.7 %broadcast_in_dim.2 = bf16[2,2,128]{2,1,0:T(2,128)(2,1)S(1)} broadcast(bf16[2]{0:T(256)(128)(2,1)} %param.3), dimensions={0} | broadcast | bytes 1028 | tf_op jit(solution)/shard_map/broadcast_in_dim | solution.py:186
  4.2 0.1 pad_maximum_fusion.2
  4.3 0.1 reshape.7
  4.4 4.8 %collective-permute-start = (bf16[4,4224]{1,0:T(4,128)(2,1)S(1)}, bf16[4,4224]{1,0:T(4,128)(2,1)S(1)}, u32[]{:S(2)}, u32[]{:S(2)}) collective-permute-start(bf16[4,4224]{1,0:T(4,128)(2,1)S(1)} %reshape.7), channel_id=1, source_target_pairs={{0,1},{1,2},{2,3},{3,4},{4,5},{5,6},{6,7},{8,9},{9,10},{10,11},{11... | collective-permute-start | bytes 101384 | tf_op jit(solution)/shard_map/ppermute | solution.py:192
  9.2 0.1 reshape.8
  9.3 1.3 %collective-permute-start.1 = (bf16[4,4224]{1,0:T(4,128)(2,1)S(1)}, bf16[4,4224]{1,0:T(4,128)(2,1)S(1)}, u32[]{:S(2)}, u32[]{:S(2)}) collective-permute-start(bf16[4,4224]{1,0:T(4,128)(2,1)S(1)} %reshape.8), channel_id=1, source_target_pairs={{1,0},{2,1},{3,2},{4,3},{5,4},{6,5},{7,6},{9,8},{10,9},{11,10},{12... | collective-permute-start | bytes 101384 | tf_op jit(solution)/shard_map/ppermute | solution.py:193
  10.6 2.8 %collective-permute-start.6 = (bf16[2,16,4096]{2,1,0:T(8,128)(2,1)S(1)}, bf16[2,16,4096]{2,1,0:T(8,128)(2,1)S(1)}, u32[]{:S(2)}, u32[]{:S(2)}) collective-permute-start(bf16[2,16,4096]{2,1,0:T(8,128)(2,1)S(1)} %copy-done), channel_id=1, source_target_pairs={{0,8},{8,16},{16,24},{24,32},{32,40},{40,48},{48,56},{56,64},{64,7... | collective-permute-start | bytes 786440 | tf_op jit(solution)/shard_map/ppermute | solution.py:176
  13.4 0.3 collective-permute-done.2.visitor_ref
  13.7 0.0 collective-permute-start.3
  13.7 0.0 collective-permute-done
  13.7 2.5 %collective-permute-done.1 = bf16[4,4224]{1,0:T(4,128)(2,1)S(1)} collective-permute-done((bf16[4,4224]{1,0:T(4,128)(2,1)S(1)}, bf16[4,4224]{1,0:T(4,128)(2,1)S(1)}, u32[]{:S(2)}, u32[]{:S(2)}) %collective-permute-start.1) | collective-permute-done | bytes 33824 | tf_op jit(solution)/shard_map/ppermute | solution.py:193
  16.3 3.2 %collective-permute-start.7 = (bf16[8,4224]{1,0:T(8,128)(2,1)S(1)}, bf16[8,4224]{1,0:T(8,128)(2,1)S(1)}, u32[]{:S(2)}, u32[]{:S(2)}) collective-permute-start(bf16[8,4224]{1,0:T(8,128)(2,1)S(1)} %pad_maximum_fusion.own_halo_ref.halo_ref), channel_id=1, source_target_pairs={{0,8},{8,16},{16,24},{24,32},{32,40},{40,48},{48,56},{56,64},{64,7... | collective-permute-start | bytes 202760 | tf_op jit(solution)/shard_map/ppermute | solution.py:176
  19.5 1.6 %collective-permute-start.5 = (bf16[8,4224]{1,0:T(8,128)(2,1)S(1)}, bf16[8,4224]{1,0:T(8,128)(2,1)S(1)}, u32[]{:S(2)}, u32[]{:S(2)}) collective-permute-start(bf16[8,4224]{1,0:T(8,128)(2,1)S(1)} %pad_maximum_fusion.own_halo_ref.halo_ref), channel_id=1, source_target_pairs={{0,16},{8,24},{16,32},{24,40},{32,48},{40,56},{48,64},{56,72},{64,... | collective-permute-start | bytes 202760 | tf_op jit(solution)/shard_map/ppermute | solution.py:176
  21.1 2.9 %collective-permute-start.4 = (bf16[8,4224]{1,0:T(8,128)(2,1)S(1)}, bf16[8,4224]{1,0:T(8,128)(2,1)S(1)}, u32[]{:S(2)}, u32[]{:S(2)}) collective-permute-start(bf16[8,4224]{1,0:T(8,128)(2,1)S(1)} %pad_maximum_fusion.own_halo_ref.halo_ref), channel_id=1, source_target_pairs={{0,24},{8,32},{16,40},{24,48},{32,56},{40,64},{48,72},{56,80},{64,... | collective-permute-start | bytes 202760 | tf_op jit(solution)/shard_map/ppermute | solution.py:176
  24.0 0.0 copy-done.1
  24.0 6.0 %visit.4.rest_0_ = f32[2,16,4096]{2,1,0:T(8,128)} custom-call(bf16[2,16,4096]{2,1,0:T(8,128)(2,1)} %own_ref.7, bf16[8,4224]{1,0:T(8,128)(2,1)} %copy-done.1, bf16[2,16,4096]{2,1,0:T(8,128)(2,1)} %own_ref.7, bf16[8,4224]{1,0:T(8,128)(2,1)} %copy-done.1), custom_call_target="tpu_custom_call" | custom-call | tf_op jit(solution)/shard_map/visit/pallas_call | solution.py:158
  30.0 0.0 collective-permute-done.7.halo_ref
  30.0 0.0 collective-permute-done.6.visitor_ref
  30.0 0.6 %copy-done.7 = bf16[8,4224]{1,0:T(8,128)(2,1)} copy-done((bf16[8,4224]{1,0:T(8,128)(2,1)}, bf16[8,4224]{1,0:T(8,128)(2,1)S(1)}, u32[]{:S(2)}) %copy-start.7) | copy-done | bytes 67608
  30.6 0.7 %copy-done.4 = bf16[2,16,4096]{2,1,0:T(8,128)(2,1)} copy-done((bf16[2,16,4096]{2,1,0:T(8,128)(2,1)}, bf16[2,16,4096]{2,1,0:T(8,128)(2,1)S(1)}, u32[]{:S(2)}) %copy-start.4) | copy-done | bytes 262168
  31.3 6.2 %visit.5.rest_0_ = f32[2,16,4096]{2,1,0:T(8,128)} custom-call(bf16[2,16,4096]{2,1,0:T(8,128)(2,1)} %own_ref.7, bf16[8,4224]{1,0:T(8,128)(2,1)} %copy-done.1, bf16[2,16,4096]{2,1,0:T(8,128)(2,1)} %copy-done.4, bf16[8,4224]{1,0:T(8,128)(2,1)} %copy-done.7, f32[2,16,4096]{2,1,0:T(8,128)} %visit.4.rest_0_), custom_call_target="tpu_custom_call", output_to_operand_aliasing={{}: (4, {})} | custom-call | tf_op jit(solution)/shard_map/visit/pallas_call | solution.py:158
  37.5 0.0 copy-done.2
  37.5 0.0 collective-permute-done.5.halo_ref
  37.5 0.6 %copy-done.6 = bf16[8,4224]{1,0:T(8,128)(2,1)} copy-done((bf16[8,4224]{1,0:T(8,128)(2,1)}, bf16[8,4224]{1,0:T(8,128)(2,1)S(1)}, u32[]{:S(2)}) %copy-start.6) | copy-done | bytes 67608
  38.2 6.2 %visit.6.rest_0_ = f32[2,16,4096]{2,1,0:T(8,128)} custom-call(bf16[2,16,4096]{2,1,0:T(8,128)(2,1)} %own_ref.7, bf16[8,4224]{1,0:T(8,128)(2,1)} %copy-done.1, bf16[2,16,4096]{2,1,0:T(8,128)(2,1)} %copy-done.2, bf16[8,4224]{1,0:T(8,128)(2,1)} %copy-done.6, f32[2,16,4096]{2,1,0:T(8,128)} %visit.5.rest_0_), custom_call_target="tpu_custom_call", output_to_operand_aliasing={{}: (4, {})} | custom-call | tf_op jit(solution)/shard_map/visit/pallas_call | solution.py:158
  44.4 0.0 collective-permute-done.4.halo_ref
  44.4 0.0 collective-permute-done.3.visitor_ref
  44.4 0.6 %copy-done.5 = bf16[8,4224]{1,0:T(8,128)(2,1)} copy-done((bf16[8,4224]{1,0:T(8,128)(2,1)}, bf16[8,4224]{1,0:T(8,128)(2,1)S(1)}, u32[]{:S(2)}) %copy-start.5) | copy-done | bytes 67608
  45.0 0.7 %copy-done.3 = bf16[2,16,4096]{2,1,0:T(8,128)(2,1)} copy-done((bf16[2,16,4096]{2,1,0:T(8,128)(2,1)}, bf16[2,16,4096]{2,1,0:T(8,128)(2,1)S(1)}, u32[]{:S(2)}) %copy-start.3) | copy-done | bytes 262168
  45.7 6.2 %visit.7 = f32[2,16,4096]{2,1,0:T(8,128)} custom-call(bf16[2,16,4096]{2,1,0:T(8,128)(2,1)} %own_ref.7, bf16[8,4224]{1,0:T(8,128)(2,1)} %copy-done.1, bf16[2,16,4096]{2,1,0:T(8,128)(2,1)} %copy-done.3, bf16[8,4224]{1,0:T(8,128)(2,1)} %copy-done.5, f32[2,16,4096]{2,1,0:T(8,128)} %visit.6.rest_0_), custom_call_target="tpu_custom_call", output_to_operand_aliasing={{}: (4, {})} | custom-call | tf_op jit(solution)/shard_map/visit/pallas_call | solution.py:158
  (10 shorter events, 0.1 us)
Async XLA Ops:
  0.0 10.6 %copy-start = (bf16[2,16,4096]{2,1,0:T(8,128)(2,1)S(1)}, bf16[2,16,4096]{2,1,0:T(8,128)(2,1)}, u32[]{:S(2)}) copy-start(bf16[2,16,4096]{2,1,0:T(8,128)(2,1)} %own_ref.7) | copy-start | bytes 786436
  0.0 13.7 %collective-permute-start.2 = (bf16[2,16,4096]{2,1,0:T(8,128)(2,1)}, bf16[2,16,4096]{2,1,0:T(8,128)(2,1)S(1)}, u32[]{:S(2)}, u32[]{:S(2)}) collective-permute-start(bf16[2,16,4096]{2,1,0:T(8,128)(2,1)} %own_ref.7), channel_id=1, source_target_pairs={{0,16},{8,24},{16,32},{24,40},{32,48},{40,56},{48,64},{56,72},{64,... | collective-permute-start | bytes 786440 | tf_op jit(solution)/shard_map/ppermute | solution.py:176
  4.4 9.4 %collective-permute-start = (bf16[4,4224]{1,0:T(4,128)(2,1)S(1)}, bf16[4,4224]{1,0:T(4,128)(2,1)S(1)}, u32[]{:S(2)}, u32[]{:S(2)}) collective-permute-start(bf16[4,4224]{1,0:T(4,128)(2,1)S(1)} %reshape.7), channel_id=1, source_target_pairs={{0,1},{1,2},{2,3},{3,4},{4,5},{5,6},{6,7},{8,9},{9,10},{10,11},{11... | collective-permute-start | bytes 101384 | tf_op jit(solution)/shard_map/ppermute | solution.py:192
  9.3 7.0 %collective-permute-start.1 = (bf16[4,4224]{1,0:T(4,128)(2,1)S(1)}, bf16[4,4224]{1,0:T(4,128)(2,1)S(1)}, u32[]{:S(2)}, u32[]{:S(2)}) collective-permute-start(bf16[4,4224]{1,0:T(4,128)(2,1)S(1)} %reshape.8), channel_id=1, source_target_pairs={{1,0},{2,1},{3,2},{4,3},{5,4},{6,5},{7,6},{9,8},{10,9},{11,10},{12... | collective-permute-start | bytes 101384 | tf_op jit(solution)/shard_map/ppermute | solution.py:193
  10.6 19.5 %collective-permute-start.6 = (bf16[2,16,4096]{2,1,0:T(8,128)(2,1)S(1)}, bf16[2,16,4096]{2,1,0:T(8,128)(2,1)S(1)}, u32[]{:S(2)}, u32[]{:S(2)}) collective-permute-start(bf16[2,16,4096]{2,1,0:T(8,128)(2,1)S(1)} %copy-done), channel_id=1, source_target_pairs={{0,8},{8,16},{16,24},{24,32},{32,40},{40,48},{48,56},{56,64},{64,7... | collective-permute-start | bytes 786440 | tf_op jit(solution)/shard_map/ppermute | solution.py:176
  13.7 23.8 %copy-start.2 = (bf16[2,16,4096]{2,1,0:T(8,128)(2,1)}, bf16[2,16,4096]{2,1,0:T(8,128)(2,1)S(1)}, u32[]{:S(2)}) copy-start(bf16[2,16,4096]{2,1,0:T(8,128)(2,1)S(1)} %collective-permute-done.2.visitor_ref) | copy-start | bytes 786436
  13.7 30.6 %collective-permute-start.3 = (bf16[2,16,4096]{2,1,0:T(8,128)(2,1)S(1)}, bf16[2,16,4096]{2,1,0:T(8,128)(2,1)S(1)}, u32[]{:S(2)}, u32[]{:S(2)}) collective-permute-start(bf16[2,16,4096]{2,1,0:T(8,128)(2,1)S(1)} %collective-permute-done.2.visitor_ref), channel_id=1, source_target_pairs={{0,8},{8,16},{16,24},{24,32},{32,40},{40,48},{48,56},{56,64},{64,7... | collective-permute-start | bytes 786440 | tf_op jit(solution)/shard_map/ppermute | solution.py:176
  16.3 7.8 %copy-start.1 = (bf16[8,4224]{1,0:T(8,128)(2,1)}, bf16[8,4224]{1,0:T(8,128)(2,1)S(1)}, u32[]{:S(2)}) copy-start(bf16[8,4224]{1,0:T(8,128)(2,1)S(1)} %pad_maximum_fusion.own_halo_ref.halo_ref) | copy-start | bytes 202756
  16.3 13.7 %collective-permute-start.7 = (bf16[8,4224]{1,0:T(8,128)(2,1)S(1)}, bf16[8,4224]{1,0:T(8,128)(2,1)S(1)}, u32[]{:S(2)}, u32[]{:S(2)}) collective-permute-start(bf16[8,4224]{1,0:T(8,128)(2,1)S(1)} %pad_maximum_fusion.own_halo_ref.halo_ref), channel_id=1, source_target_pairs={{0,8},{8,16},{16,24},{24,32},{32,40},{40,48},{48,56},{56,64},{64,7... | collective-permute-start | bytes 202760 | tf_op jit(solution)/shard_map/ppermute | solution.py:176
  19.5 18.1 %collective-permute-start.5 = (bf16[8,4224]{1,0:T(8,128)(2,1)S(1)}, bf16[8,4224]{1,0:T(8,128)(2,1)S(1)}, u32[]{:S(2)}, u32[]{:S(2)}) collective-permute-start(bf16[8,4224]{1,0:T(8,128)(2,1)S(1)} %pad_maximum_fusion.own_halo_ref.halo_ref), channel_id=1, source_target_pairs={{0,16},{8,24},{16,32},{24,40},{32,48},{40,56},{48,64},{56,72},{64,... | collective-permute-start | bytes 202760 | tf_op jit(solution)/shard_map/ppermute | solution.py:176
  21.1 23.3 %collective-permute-start.4 = (bf16[8,4224]{1,0:T(8,128)(2,1)S(1)}, bf16[8,4224]{1,0:T(8,128)(2,1)S(1)}, u32[]{:S(2)}, u32[]{:S(2)}) collective-permute-start(bf16[8,4224]{1,0:T(8,128)(2,1)S(1)} %pad_maximum_fusion.own_halo_ref.halo_ref), channel_id=1, source_target_pairs={{0,24},{8,32},{16,40},{24,48},{32,56},{40,64},{48,72},{56,80},{64,... | collective-permute-start | bytes 202760 | tf_op jit(solution)/shard_map/ppermute | solution.py:176
  30.0 0.6 %copy-start.7 = (bf16[8,4224]{1,0:T(8,128)(2,1)}, bf16[8,4224]{1,0:T(8,128)(2,1)S(1)}, u32[]{:S(2)}) copy-start(bf16[8,4224]{1,0:T(8,128)(2,1)S(1)} %collective-permute-done.7.halo_ref) | copy-start | bytes 202756
  30.6 0.7 %copy-start.4 = (bf16[2,16,4096]{2,1,0:T(8,128)(2,1)}, bf16[2,16,4096]{2,1,0:T(8,128)(2,1)S(1)}, u32[]{:S(2)}) copy-start(bf16[2,16,4096]{2,1,0:T(8,128)(2,1)S(1)} %collective-permute-done.6.visitor_ref) | copy-start | bytes 786436
  37.5 0.6 %copy-start.6 = (bf16[8,4224]{1,0:T(8,128)(2,1)}, bf16[8,4224]{1,0:T(8,128)(2,1)S(1)}, u32[]{:S(2)}) copy-start(bf16[8,4224]{1,0:T(8,128)(2,1)S(1)} %collective-permute-done.5.halo_ref) | copy-start | bytes 202756
  44.4 0.6 %copy-start.5 = (bf16[8,4224]{1,0:T(8,128)(2,1)}, bf16[8,4224]{1,0:T(8,128)(2,1)S(1)}, u32[]{:S(2)}) copy-start(bf16[8,4224]{1,0:T(8,128)(2,1)S(1)} %collective-permute-done.4.halo_ref) | copy-start | bytes 202756
  45.0 0.7 %copy-start.3 = (bf16[2,16,4096]{2,1,0:T(8,128)(2,1)}, bf16[2,16,4096]{2,1,0:T(8,128)(2,1)S(1)}, u32[]{:S(2)}) copy-start(bf16[2,16,4096]{2,1,0:T(8,128)(2,1)S(1)} %collective-permute-done.3.visitor_ref) | copy-start | bytes 786436

commit v2 on v0

v2 whole, which is shorter than its diff:
```python
import math

import jax
import jax.numpy as jnp
from jax import lax
from jax.experimental import pallas as pl
from jax.experimental.pallas import tpu as pltpu
from jax.sharding import PartitionSpec as P


NZ = 64
LANES = 128
UNROLL_RHO = 8
UNROLL_MID = 16
UNROLL_OUT = 16

screening = 0.5
ratio_mid = (12.0 + 2.0 * screening) / 12.0
root_term = math.sqrt(ratio_mid * ratio_mid - 1.0)
decay_ratio = ratio_mid - root_term
coeff_zero = 1.0 / (6.0 * root_term)
coeff_one = -2.0 * decay_ratio * coeff_zero
coeff_two = 2.0 * decay_ratio * decay_ratio * coeff_zero

lead = coeff_two / 18.0
slope = (-coeff_one / 6.0) / lead
base = (coeff_zero - coeff_two) / lead

SHAPE = (8, LANES)
PAIRS = ((0, 0), (1, 1), (0, 1), (1, 0))


def lanes_by(v, k):
    return pltpu.roll(v, k % LANES, axis=1)


def rows_by(v, k):
    return pltpu.roll(v, k % 8, axis=0)


def iotas():
    return lax.broadcasted_iota(jnp.int32, SHAPE, 0), lax.broadcasted_iota(jnp.int32, SHAPE, 1)


def columns(g):
    return pl.ds(pl.multiple_of(g * LANES, LANES), LANES)


def planes_of(ref, i, g):
    v = ref[i, :, columns(g)].astype(jnp.float32)
    return v[:8], v[8:]


def at_row(at, e, by=0):
    return pl.ds(24 * at + 8 + 8 * e + by, 8)


def sweep(step, groups, unroll):
    def body(n, carry):
        for k in range(unroll):
            step(n * unroll + k)
        return carry

    lax.fori_loop(0, groups // unroll, body, 0)


def transverse(v, about_y, at, k, masks):
    low, has_left, has_right = masks
    left = jnp.where(has_left, lanes_by(v, 1), 0.0)
    right = jnp.where(has_right, lanes_by(v, -1), 0.0)
    across = jnp.where(low, about_y[at - 1, k], about_y[at + 1, k])
    return (about_y[at, k] + across) + (left + right)


def lane_masks(lane):
    return lane < NZ, lane % NZ != 0, lane % NZ != NZ - 1


def prepare_kernel(orbitals_ref, occupation_ref, wide_ref, first_ref, second_ref, *, even_of):
    cells = orbitals_ref.shape[2]
    planes = orbitals_ref.shape[1]
    wide_ref[:, :, :cells] = orbitals_ref[...]
    even = even_of()
    row = lax.broadcasted_iota(jnp.int32, (4, LANES), 0)
    weights = [occupation_ref[j].astype(jnp.float32) for j in range(2)]
    for j in range(2):
        wide_ref[j, :, cells:] = jnp.full((planes, LANES), weights[j], jnp.float32).astype(jnp.bfloat16)
    tail = jnp.where(row < 2, weights[0], weights[1]).astype(jnp.bfloat16)
    first_ref[:, cells:] = tail
    second_ref[:, cells:] = tail

    def step(g):
        v = [orbitals_ref[j, :, columns(g)].astype(jnp.float32) for j in range(2)]

        def rows(a, b):
            return jnp.concatenate([v[0][a : a + 1], v[0][b : b + 1], v[1][a : a + 1], v[1][b : b + 1]], axis=0)

        high, leading = rows(planes - 1, planes - 2), rows(1, 0)
        first_ref[:, columns(g)] = jnp.where(even, high, leading).astype(jnp.bfloat16)
        second_ref[:, columns(g)] = jnp.where(even, leading, high).astype(jnp.bfloat16)

    sweep(step, cells // LANES, 8)


def visit_kernel(own_ref, visitor_ref, *rest):
    running_ref = rest[0] if len(rest) == 4 else None
    out_ref, rho, mid = rest[-3:]
    groups = out_ref.shape[2] // LANES
    lane = iotas()[1]
    high, has_left, has_right = lane >= NZ, lane % NZ != 0, lane % NZ != NZ - 1
    zero = jnp.zeros(SHAPE, jnp.float32)
    weight = []
    for j in range(2):
        w = visitor_ref[j, :, groups * LANES :].astype(jnp.float32)
        weight.append(w[:8] * -lead)
    for ref in (rho, mid):
        for at in range(4):
            for e in range(2):
                ref[0, at_row(at, e), :] = zero
                ref[groups + 1, at_row(at, e), :] = zero

    def stencil(ref, g, at, e, v):
        left = jnp.where(has_left, lanes_by(v, 1), 0.0)
        right = jnp.where(has_right, lanes_by(v, -1), 0.0)
        rows = at_row(at, e)
        about = lanes_by(v + jnp.where(high, ref[g, rows, :], ref[g + 2, rows, :]), NZ)
        x = ref[g + 1, at_row(at, e, -1), :] + ref[g + 1, at_row(at, e, 1), :]
        return (x + about) + (left + right)

    def step_rho(g):
        own = [planes_of(own_ref, i, g) for i in range(2)]
        vis = [planes_of(visitor_ref, j, g) for j in range(2)]
        for n in range(5):
            rho[g + 1, pl.ds(24 * n, 8), :] = zero
            mid[g + 1, pl.ds(24 * n, 8), :] = zero
        for at, (i, j) in enumerate(PAIRS):
            for e in range(2):
                rho[g + 1, at_row(at, e), :] = own[i][e] * vis[j][e]

    def step_mid(g):
        for at in range(4):
            for e in range(2):
                v = rho[g + 1, at_row(at, e), :]
                mid[g + 1, at_row(at, e), :] = v * slope + stencil(rho, g, at, e, v)

    def step_out(g):
        vis = [planes_of(visitor_ref, j, g) for j in range(2)]
        for i in range(2):
            for e in range(2):
                total = None
                for at in range(4):
                    if PAIRS[at][0] == i:
                        v = mid[g + 1, at_row(at, e), :]
                        pot = rho[g + 1, at_row(at, e), :] * base + stencil(mid, g, at, e, v)
                        j = PAIRS[at][1]
                        term = (weight[j] * vis[j][e]) * pot
                        total = term if total is None else total + term
                if running_ref is not None:
                    total = total + running_ref[i, 8 * e : 8 * e + 8, columns(g)]
                out_ref[i, 8 * e : 8 * e + 8, columns(g)] = total

    sweep(step_rho, groups, UNROLL_RHO)
    sweep(step_mid, groups, UNROLL_MID)
    sweep(step_out, groups, UNROLL_OUT)


def edge_kernel(own_ref, own_halo_ref, *rest):
    out_ref, rho, rho_y = rest[-3:]
    running_ref = rest[-4]
    visitors = rest[: (len(rest) - 4) // 2]
    halos = rest[(len(rest) - 4) // 2 : -4]
    groups = out_ref.shape[2] // LANES
    row, lane = iotas()
    masks = lane_masks(lane)
    zero = jnp.zeros(SHAPE, jnp.float32)
    inside = own_halo_ref[:, groups * LANES :].astype(jnp.float32) > 0.0
    nearest = (row == 0) | (row == 2) | (row == 5) | (row == 7)
    near_inside = nearest & inside
    even_row = row % 2 == 0
    upper = row % 4 < 2

    def swap(v):
        return jnp.where(upper, rows_by(v, -2), rows_by(v, 2))

    def edges(ref, g):
        a0, a1 = planes_of(ref, 0, g)
        b0, b1 = planes_of(ref, 1, g)
        return jnp.where(row < 2, a0, jnp.where(row < 4, rows_by(b0, 2), jnp.where(row < 6, rows_by(a1, -2), b1)))

    weight = []
    for ref in visitors:
        w0 = ref[0, :, groups * LANES :].astype(jnp.float32)[:8]
        w1 = ref[1, :, groups * LANES :].astype(jnp.float32)[:8]
        weight.append(jnp.where(upper, w0, w1) * -lead)
    for k in range(2 * len(visitors)):
        rho_y[0, k] = zero
        rho_y[groups + 1, k] = zero

    def step_rho(g):
        oh = own_halo_ref[:, columns(g)].astype(jnp.float32)
        for n, ref in enumerate(halos):
            vh = ref[:, columns(g)].astype(jnp.float32)
            for k, v in ((2 * n, oh * vh), (2 * n + 1, oh * swap(vh))):
                rho[g, k] = v
                rho_y[g + 1, k] = lanes_by(v, NZ)

    def step_out(g):
        oe = edges(own_ref, g)
        total = None
        for n, ref in enumerate(visitors):
            ve = edges(ref, g)
            we = ve * weight[n]
            for k, ve, we in ((2 * n, ve, we), (2 * n + 1, swap(ve), swap(we))):
                v = rho[g, k]
                beside = jnp.where(even_row, rows_by(v, -1), rows_by(v, 1))
                t = transverse(v, rho_y, g + 1, k, masks)
                t = jnp.where(nearest, v * slope + (t + t), 0.0) + jnp.where(near_inside, oe * ve, 0.0)
                term = we * (beside + t)
                total = term if total is None else total + term
        for i in range(2):
            low_planes = running_ref[i, :8, columns(g)]
            out_ref[i, :8, columns(g)] = low_planes + jnp.where(row < 2, total if i == 0 else rows_by(total, -2), 0.0)
            high_planes = running_ref[i, 8:, columns(g)]
            out_ref[i, 8:, columns(g)] = high_planes + jnp.where(row >= 6, rows_by(total, 2) if i == 0 else total, 0.0)

    sweep(step_rho, groups, 32)
    sweep(step_out, groups, 16)


VMEM = pl.BlockSpec(memory_space=pltpu.VMEM)


def in_vmem(x):
    return pltpu.with_memory_space_constraint(x, pltpu.VMEM)


def prepare(orbitals, occupation, even_of):
    cells = orbitals.shape[2]
    return pl.pallas_call(
        lambda *refs: prepare_kernel(*refs, even_of=even_of),
        out_shape=[
            pltpu.VMEM((*orbitals.shape[:2], cells + LANES), orbitals.dtype),
            pltpu.VMEM((4, cells + LANES), orbitals.dtype),
            pltpu.VMEM((4, cells + LANES), orbitals.dtype),
        ],
        in_specs=[VMEM, pl.BlockSpec(memory_space=pltpu.SMEM)],
        out_specs=[VMEM] * 3,
        name="prepare",
    )(orbitals, occupation)


def visit(own, visitor, running):
    shape = (*own.shape[:2], own.shape[2] - LANES)
    groups = shape[2] // LANES
    operands = [in_vmem(x) for x in (own, visitor) + (() if running is None else (running,))]
    held = pltpu.VMEM((groups + 2, 104, LANES), jnp.float32)
    return pl.pallas_call(
        visit_kernel,
        out_shape=pltpu.VMEM(shape, jnp.float32),
        in_specs=[VMEM] * len(operands),
        out_specs=VMEM,
        scratch_shapes=[held, held],
        name="visit",
    )(*operands)


def finish(own, own_halo, visitors, halos, running):
    groups = running.shape[2] // LANES
    count = 2 * len(visitors)
    operands = [in_vmem(x) for x in (own, own_halo, *visitors, *halos, running)]
    return pl.pallas_call(
        edge_kernel,
        out_shape=jax.ShapeDtypeStruct(running.shape, jnp.float32),
        in_specs=[VMEM] * len(operands),
        out_specs=VMEM,
        scratch_shapes=[
            pltpu.VMEM((groups, count, *SHAPE), jnp.float32),
            pltpu.VMEM((groups + 2, count, *SHAPE), jnp.float32),
        ],
        name="finish",
    )(*operands)


def from_two_back(array):
    size = lax.axis_size("band")
    return lax.ppermute(array, "band", [(i, (i + 2) % size) for i in range(size)])


def across_pair_and_three(array):
    size = lax.axis_size("band")
    return lax.ppermute(array, "band", [(i, (i + 1 + 2 * (i % 2)) % size) for i in range(size)])


def swapped_in_pair(array):
    size = lax.axis_size("band")
    return lax.ppermute(array, "band", [(i, i ^ 1) for i in range(size)])


def per_device(orbitals, occupation):
    size = lax.axis_size("slab")
    even = lax.axis_index("slab") % 2 == 0
    wide, first, second = prepare(orbitals, occupation, lambda: lax.axis_index("slab") % 2 == 0)
    beside_second = lax.ppermute(second, "slab", [(i, ((i - 1) ^ 1) + 1) for i in range(1, size - 1)])
    beside_first = lax.ppermute(first, "slab", [(i, i ^ 1) for i in range(size)])
    two_back = from_two_back(wide)
    other = across_pair_and_three(wide)
    swapped = swapped_in_pair(two_back)
    halo = jnp.concatenate([jnp.where(even, beside_second, beside_first), jnp.where(even, beside_first, beside_second)], axis=0)
    halo_two = from_two_back(halo)
    halo_other = across_pair_and_three(halo)
    halo_swapped = swapped_in_pair(halo_two)
    running = visit(wide, wide, None)
    running = visit(wide, two_back, running)
    running = visit(wide, swapped, running)
    running = visit(wide, other, running)
    return finish(wide, halo, (wide, two_back, swapped, other), (halo, halo_two, halo_swapped, halo_other), running)


def solution(mesh):
    return jax.shard_map(
        per_device,
        mesh=mesh,
        in_specs=(P("band", "slab", None), P("band")),
        out_specs=P("band", "slab", None),
        check_vma=False,
    )
```

time: 104 us -> 46.1 us (0.44)
  the two profiles are of different devices: /device:TPU:16 before, /device:TPU:1 now
where the time goes in v2:
time: 46.1 us; the launch traced here: 45.9 us
  starting transfers between devices  18.1 us (39%)
  waiting for transfers between devices  15.9 us (34%)
  Pallas kernels  11.8 us (26%)
    ppermute x2, waiting for transfers between devices, from_two_back(): lax.ppermute(array, 'band', [(i, (i + 2) % size) for i in range(size)])  15.9 us
    pallas_call x4, Pallas kernels, visit(): pl.pallas_call(visit_kernel, out_shape=pltpu.VMEM(shape, jnp.float32), in...  8.49 us
    ppermute x2, starting transfers between devices, across_pair_and_three(): lax.ppermute(array, 'band', [(i, (i + 1 + 2 * (i % 2)) % size) for i in r...  6.79 us
    ppermute x1, starting transfers between devices, per_device(): lax.ppermute(first, 'slab', [(i, i ^ 1) for i in range(size)])  6.05 us
    ppermute x2, starting transfers between devices, swapped_in_pair(): return lax.ppermute(array, 'band', [(i, i ^ 1) for i in range(size)])  2.86 us
    pallas_call x1, Pallas kernels, finish(): pl.pallas_call(edge_kernel, out_shape=jax.ShapeDtypeStruct(running.shape,...  2.2 us
    ppermute x2, starting transfers between devices, from_two_back(): lax.ppermute(array, 'band', [(i, (i + 2) % size) for i in range(size)])  1.72 us
    pallas_call x1, Pallas kernels, prepare(): pl.pallas_call(lambda *refs: prepare_kernel(*refs, even_of=even_of), out_...  1.1 us
  transfers between devices with their start and end apart: 8, of which 2 were waited for; matrix products, arithmetic and copies ran while one was open for 0% of the time, Pallas kernels for 18%

profile of v2, /device:TPU:1, one launch (start us, length us, event | category | flops | bytes accessed | tf_op | source)
XLA Modules:
  0.0 45.9 jit_solution(5605234521969149085)
XLA Ops:
  0.0 1.1 %prepare.1 = (bf16[2,16,4224]{2,1,0:T(8,128)(2,1)S(1)}, bf16[4,4224]{1,0:T(4,128)(2,1)S(1)}, bf16[4,4224]{1,0:T(4,128)(2,1)S(1)}) custom-call(bf16[2,16,4096]{2,1,0:T(8,128)(2,1)} %refs_0_.1, bf16[2]{0:T(256)(128)(2,1)} %refs_1_.1), custom_call_target="tpu_custom_call" | custom-call | tf_op jit(solution)/shard_map/prepare/pallas_call | solution.py:239
  1.1 0.7 %collective-permute-start = (bf16[4,4224]{1,0:T(4,128)(2,1)S(1)}, bf16[4,4224]{1,0:T(4,128)(2,1)S(1)}, u32[]{:S(2)}, u32[]{:S(2)}) collective-permute-start(bf16[4,4224]{1,0:T(4,128)(2,1)S(1)} %get-tuple-element.9), channel_id=1, source_target_pairs={{1,2},{2,1},{3,4},{4,3},{5,6},{6,5},{9,10},{10,9},{11,12},{12,11},... | collective-permute-start | bytes 101384 | tf_op jit(solution)/shard_map/ppermute | solution.py:303
  1.8 6.0 %collective-permute-start.1 = (bf16[4,4224]{1,0:T(4,128)(2,1)S(1)}, bf16[4,4224]{1,0:T(4,128)(2,1)S(1)}, u32[]{:S(2)}, u32[]{:S(2)}) collective-permute-start(bf16[4,4224]{1,0:T(4,128)(2,1)S(1)} %get-tuple-element.10), channel_id=1, source_target_pairs={{0,1},{1,0},{2,3},{3,2},{4,5},{5,4},{6,7},{7,6},{8,9},{9,8},{10,11... | collective-permute-start | bytes 101384 | tf_op jit(solution)/shard_map/ppermute | solution.py:304
  7.8 4.1 %collective-permute-start.4 = (bf16[2,16,4224]{2,1,0:T(8,128)(2,1)S(1)}, bf16[2,16,4224]{2,1,0:T(8,128)(2,1)S(1)}, u32[]{:S(2)}, u32[]{:S(2)}) collective-permute-start(bf16[2,16,4224]{2,1,0:T(8,128)(2,1)S(1)} %get-tuple-element.8.own_ref.visitor_ref.rest_0_), channel_id=1, source_target_pairs={{0,8},{8,32},{16,24},{24,48},{32,40},{40,64},{48,56},{56,80},{64,7... | collective-permute-start | bytes 811016 | tf_op jit(solution)/shard_map/ppermute | solution.py:291
  11.9 1.6 %collective-permute-start.2 = (bf16[2,16,4224]{2,1,0:T(8,128)(2,1)S(1)}, bf16[2,16,4224]{2,1,0:T(8,128)(2,1)S(1)}, u32[]{:S(2)}, u32[]{:S(2)}) collective-permute-start(bf16[2,16,4224]{2,1,0:T(8,128)(2,1)S(1)} %get-tuple-element.8.own_ref.visitor_ref.rest_0_), channel_id=1, source_target_pairs={{0,16},{8,24},{16,32},{24,40},{32,48},{40,56},{48,64},{56,72},{64,... | collective-permute-start | bytes 811016 | tf_op jit(solution)/shard_map/ppermute | solution.py:286
  13.6 0.0 collective-permute-done
  13.6 0.0 collective-permute-done.1
  13.6 13.3 %collective-permute-done.2.visitor_ref.rest_1_ = bf16[2,16,4224]{2,1,0:T(8,128)(2,1)S(1)} collective-permute-done((bf16[2,16,4224]{2,1,0:T(8,128)(2,1)S(1)}, bf16[2,16,4224]{2,1,0:T(8,128)(2,1)S(1)}, u32[]{:S(2)}, u32[]{:S(2)}) %collective-permute-start.2) | collective-permute-done | bytes 270368 | tf_op jit(solution)/shard_map/ppermute | solution.py:286
  26.9 0.0 collective-permute-start.3
  27.0 0.1 collective-permute-start.5
  27.1 2.7 %collective-permute-start.7 = (bf16[8,4224]{1,0:T(8,128)(2,1)S(1)}, bf16[8,4224]{1,0:T(8,128)(2,1)S(1)}, u32[]{:S(2)}, u32[]{:S(2)}) collective-permute-start(bf16[8,4224]{1,0:T(8,128)(2,1)S(1)} %pad_maximum_fusion.own_halo_ref.rest_4_), channel_id=1, source_target_pairs={{0,8},{8,32},{16,24},{24,48},{32,40},{40,64},{48,56},{56,80},{64,7... | collective-permute-start | bytes 202760 | tf_op jit(solution)/shard_map/ppermute | solution.py:291
  29.8 2.6 %collective-permute-done.5.rest_5_ = bf16[8,4224]{1,0:T(8,128)(2,1)S(1)} collective-permute-done((bf16[8,4224]{1,0:T(8,128)(2,1)S(1)}, bf16[8,4224]{1,0:T(8,128)(2,1)S(1)}, u32[]{:S(2)}, u32[]{:S(2)}) %collective-permute-start.5) | collective-permute-done | bytes 67616 | tf_op jit(solution)/shard_map/ppermute | solution.py:286
  32.3 2.9 %collective-permute-start.6 = (bf16[8,4224]{1,0:T(8,128)(2,1)S(1)}, bf16[8,4224]{1,0:T(8,128)(2,1)S(1)}, u32[]{:S(2)}, u32[]{:S(2)}) collective-permute-start(bf16[8,4224]{1,0:T(8,128)(2,1)S(1)} %collective-permute-done.5.rest_5_), channel_id=1, source_target_pairs={{0,8},{8,0},{16,24},{24,16},{32,40},{40,32},{48,56},{56,48},{64,72... | collective-permute-start | bytes 202760 | tf_op jit(solution)/shard_map/ppermute | solution.py:296
  35.2 2.1 %visit.4.rest_0_ = f32[2,16,4096]{2,1,0:T(8,128)S(1)} custom-call(bf16[2,16,4224]{2,1,0:T(8,128)(2,1)S(1)} %get-tuple-element.8.own_ref.visitor_ref.rest_0_, bf16[2,16,4224]{2,1,0:T(8,128)(2,1)S(1)} %get-tuple-element.8.own_ref.visitor_ref.rest_0_), custom_call_target="tpu_custom_call" | custom-call | tf_op jit(solution)/shard_map/visit/pallas_call | solution.py:257
  37.3 2.1 %visit.5.rest_0_ = f32[2,16,4096]{2,1,0:T(8,128)S(1)} custom-call(bf16[2,16,4224]{2,1,0:T(8,128)(2,1)S(1)} %get-tuple-element.8.own_ref.visitor_ref.rest_0_, bf16[2,16,4224]{2,1,0:T(8,128)(2,1)S(1)} %collective-permute-done.2.visitor_ref.rest_1_, f32[2,16,4096]{2,1,0:T(8,128)S(1)} %visit.4.rest_0_), custom_call_target="tpu_custom_call" | custom-call | tf_op jit(solution)/shard_map/visit/pallas_call | solution.py:257
  39.4 0.0 collective-permute-done.3.visitor_ref.rest_2_
  39.4 2.1 %visit.6.rest_0_ = f32[2,16,4096]{2,1,0:T(8,128)S(1)} custom-call(bf16[2,16,4224]{2,1,0:T(8,128)(2,1)S(1)} %get-tuple-element.8.own_ref.visitor_ref.rest_0_, bf16[2,16,4224]{2,1,0:T(8,128)(2,1)S(1)} %collective-permute-done.3.visitor_ref.rest_2_, f32[2,16,4096]{2,1,0:T(8,128)S(1)} %visit.5.rest_0_), custom_call_target="tpu_custom_call" | custom-call | tf_op jit(solution)/shard_map/visit/pallas_call | solution.py:257
  41.6 0.0 collective-permute-done.4.visitor_ref.rest_3_
  41.6 2.1 %visit.7.rest_8_ = f32[2,16,4096]{2,1,0:T(8,128)S(1)} custom-call(bf16[2,16,4224]{2,1,0:T(8,128)(2,1)S(1)} %get-tuple-element.8.own_ref.visitor_ref.rest_0_, bf16[2,16,4224]{2,1,0:T(8,128)(2,1)S(1)} %collective-permute-done.4.visitor_ref.rest_3_, f32[2,16,4096]{2,1,0:T(8,128)S(1)} %visit.6.rest_0_), custom_call_target="tpu_custom_call" | custom-call | tf_op jit(solution)/shard_map/visit/pallas_call | solution.py:257
  43.7 0.0 collective-permute-done.7.rest_7_
  43.7 0.0 collective-permute-done.6.rest_6_
  43.7 2.2 %finish.1 = f32[2,16,4096]{2,1,0:T(8,128)} custom-call(bf16[2,16,4224]{2,1,0:T(8,128)(2,1)S(1)} %get-tuple-element.8.own_ref.visitor_ref.rest_0_, bf16[8,4224]{1,0:T(8,128)(2,1)S(1)} %pad_maximum_fusion.own_halo_ref.rest_4_, bf16[2,16,4224]{2,1,0:T(8,128)(2,1)S(1)} %get-tuple-element.8.own_ref.visitor_ref.rest_0_, ...), custom_call_target="tpu_custom_call" | custom-call | tf_op jit(solution)/shard_map/finish/pallas_call | solution.py:271
  (2 shorter events, 0.1 us)
Async XLA Ops:
  1.1 12.5 %collective-permute-start = (bf16[4,4224]{1,0:T(4,128)(2,1)S(1)}, bf16[4,4224]{1,0:T(4,128)(2,1)S(1)}, u32[]{:S(2)}, u32[]{:S(2)}) collective-permute-start(bf16[4,4224]{1,0:T(4,128)(2,1)S(1)} %get-tuple-element.9), channel_id=1, source_target_pairs={{1,2},{2,1},{3,4},{4,3},{5,6},{6,5},{9,10},{10,9},{11,12},{12,11},... | collective-permute-start | bytes 101384 | tf_op jit(solution)/shard_map/ppermute | solution.py:303
  1.8 11.8 %collective-permute-start.1 = (bf16[4,4224]{1,0:T(4,128)(2,1)S(1)}, bf16[4,4224]{1,0:T(4,128)(2,1)S(1)}, u32[]{:S(2)}, u32[]{:S(2)}) collective-permute-start(bf16[4,4224]{1,0:T(4,128)(2,1)S(1)} %get-tuple-element.10), channel_id=1, source_target_pairs={{0,1},{1,0},{2,3},{3,2},{4,5},{5,4},{6,7},{7,6},{8,9},{9,8},{10,11... | collective-permute-start | bytes 101384 | tf_op jit(solution)/shard_map/ppermute | solution.py:304
  7.8 33.8 %collective-permute-start.4 = (bf16[2,16,4224]{2,1,0:T(8,128)(2,1)S(1)}, bf16[2,16,4224]{2,1,0:T(8,128)(2,1)S(1)}, u32[]{:S(2)}, u32[]{:S(2)}) collective-permute-start(bf16[2,16,4224]{2,1,0:T(8,128)(2,1)S(1)} %get-tuple-element.8.own_ref.visitor_ref.rest_0_), channel_id=1, source_target_pairs={{0,8},{8,32},{16,24},{24,48},{32,40},{40,64},{48,56},{56,80},{64,7... | collective-permute-start | bytes 811016 | tf_op jit(solution)/shard_map/ppermute | solution.py:291
  11.9 15.0 %collective-permute-start.2 = (bf16[2,16,4224]{2,1,0:T(8,128)(2,1)S(1)}, bf16[2,16,4224]{2,1,0:T(8,128)(2,1)S(1)}, u32[]{:S(2)}, u32[]{:S(2)}) collective-permute-start(bf16[2,16,4224]{2,1,0:T(8,128)(2,1)S(1)} %get-tuple-element.8.own_ref.visitor_ref.rest_0_), channel_id=1, source_target_pairs={{0,16},{8,24},{16,32},{24,40},{32,48},{40,56},{48,64},{56,72},{64,... | collective-permute-start | bytes 811016 | tf_op jit(solution)/shard_map/ppermute | solution.py:286
  26.9 12.5 %collective-permute-start.3 = (bf16[2,16,4224]{2,1,0:T(8,128)(2,1)S(1)}, bf16[2,16,4224]{2,1,0:T(8,128)(2,1)S(1)}, u32[]{:S(2)}, u32[]{:S(2)}) collective-permute-start(bf16[2,16,4224]{2,1,0:T(8,128)(2,1)S(1)} %collective-permute-done.2.visitor_ref.rest_1_), channel_id=1, source_target_pairs={{0,8},{8,0},{16,24},{24,16},{32,40},{40,32},{48,56},{56,48},{64,72... | collective-permute-start | bytes 811016 | tf_op jit(solution)/shard_map/ppermute | solution.py:296
  27.0 5.3 %collective-permute-start.5 = (bf16[8,4224]{1,0:T(8,128)(2,1)S(1)}, bf16[8,4224]{1,0:T(8,128)(2,1)S(1)}, u32[]{:S(2)}, u32[]{:S(2)}) collective-permute-start(bf16[8,4224]{1,0:T(8,128)(2,1)S(1)} %pad_maximum_fusion.own_halo_ref.rest_4_), channel_id=1, source_target_pairs={{0,16},{8,24},{16,32},{24,40},{32,48},{40,56},{48,64},{56,72},{64,... | collective-permute-start | bytes 202760 | tf_op jit(solution)/shard_map/ppermute | solution.py:286
  27.1 16.6 %collective-permute-start.7 = (bf16[8,4224]{1,0:T(8,128)(2,1)S(1)}, bf16[8,4224]{1,0:T(8,128)(2,1)S(1)}, u32[]{:S(2)}, u32[]{:S(2)}) collective-permute-start(bf16[8,4224]{1,0:T(8,128)(2,1)S(1)} %pad_maximum_fusion.own_halo_ref.rest_4_), channel_id=1, source_target_pairs={{0,8},{8,32},{16,24},{24,48},{32,40},{40,64},{48,56},{56,80},{64,7... | collective-permute-start | bytes 202760 | tf_op jit(solution)/shard_map/ppermute | solution.py:291
  32.3 11.4 %collective-permute-start.6 = (bf16[8,4224]{1,0:T(8,128)(2,1)S(1)}, bf16[8,4224]{1,0:T(8,128)(2,1)S(1)}, u32[]{:S(2)}, u32[]{:S(2)}) collective-permute-start(bf16[8,4224]{1,0:T(8,128)(2,1)S(1)} %collective-permute-done.5.rest_5_), channel_id=1, source_target_pairs={{0,8},{8,0},{16,24},{24,16},{32,40},{40,32},{48,56},{56,48},{64,72... | collective-permute-start | bytes 202760 | tf_op jit(solution)/shard_map/ppermute | solution.py:296

commit v3 on v2

--- a/solution.py
+++ b/solution.py
@@ -11,8 +11,7 @@
 NZ = 64
 LANES = 128
 UNROLL_RHO = 8
-UNROLL_MID = 16
-UNROLL_OUT = 16
+CHUNK = 32
 
 screening = 0.5
 ratio_mid = (12.0 + 2.0 * screening) / 12.0
@@ -102,12 +101,24 @@
     sweep(step, cells // LANES, 8)
 
 
-def visit_kernel(own_ref, visitor_ref, *rest):
-    running_ref = rest[0] if len(rest) == 4 else None
-    out_ref, rho, mid = rest[-3:]
+def neighbour_table():
+    size = (2 * LANES, 2 * LANES)
+    a, b = (lax.broadcasted_iota(jnp.int32, size, d) for d in range(2))
+    apart = jnp.abs(a - b)
+    near = (apart == NZ) | ((apart == 1) & (a // NZ == b // NZ))
+    return jnp.where(near, 1.0, 0.0).astype(jnp.bfloat16)
+
+
+def visit_kernel(*refs):
+    first = len(refs) == 6
+    own_ref, visitor_ref = refs[:2]
+    if first:
+        out_ref, table_ref, rho, mid = refs[2:]
+        table_ref[...] = neighbour_table()
+    else:
+        running_ref, table_ref, out_ref, rho, mid = refs[2:]
     groups = out_ref.shape[2] // LANES
-    lane = iotas()[1]
-    high, has_left, has_right = lane >= NZ, lane % NZ != 0, lane % NZ != NZ - 1
+    low = iotas()[1] < NZ
     zero = jnp.zeros(SHAPE, jnp.float32)
     weight = []
     for j in range(2):
@@ -119,13 +130,32 @@
                 ref[0, at_row(at, e), :] = zero
                 ref[groups + 1, at_row(at, e), :] = zero
 
-    def stencil(ref, g, at, e, v):
-        left = jnp.where(has_left, lanes_by(v, 1), 0.0)
-        right = jnp.where(has_right, lanes_by(v, -1), 0.0)
-        rows = at_row(at, e)
-        about = lanes_by(v + jnp.where(high, ref[g, rows, :], ref[g + 2, rows, :]), NZ)
-        x = ref[g + 1, at_row(at, e, -1), :] + ref[g + 1, at_row(at, e, 1), :]
-        return (x + about) + (left + right)
+    def stencils(ref, g0, count):
+        rows = []
+        for q in range(0, count, 2):
+            for at in range(4):
+                both = [ref[g0 + q + 1 + h, pl.ds(24 * at + 8, 16), :] for h in range(2)]
+                rows.append(jnp.concatenate(both, axis=1))
+        v = jnp.concatenate(rows, axis=0)
+        coarse = v.astype(jnp.bfloat16)
+        fine = (v - coarse.astype(jnp.float32)).astype(jnp.bfloat16)
+        table = table_ref[...]
+        inner = jnp.dot(coarse, table, preferred_element_type=jnp.float32)
+        inner = inner + jnp.dot(fine, table, preferred_element_type=jnp.float32)
+        result = {}
+        for q in range(0, count, 2):
+            for at in range(4):
+                for e in range(2):
+                    g = g0 + q + 1
+                    rows = at_row(at, e)
+                    outer = lanes_by(jnp.where(low, ref[g + 2, rows, :], ref[g - 1, rows, :]), NZ)
+                    for h in range(2):
+                        x = ref[g + h, at_row(at, e, -1), :] + ref[g + h, at_row(at, e, 1), :]
+                        r = 32 * q + 16 * at + 8 * e
+                        yz = inner[r : r + 8, LANES * h : LANES * h + LANES]
+                        edge = jnp.where(low if h == 0 else ~low, outer, 0.0)
+                        result[q + h, at, e] = (x + edge) + yz
+        return result
 
     def step_rho(g):
         own = [planes_of(own_ref, i, g) for i in range(2)]
@@ -137,31 +167,34 @@
             for e in range(2):
                 rho[g + 1, at_row(at, e), :] = own[i][e] * vis[j][e]
 
-    def step_mid(g):
-        for at in range(4):
-            for e in range(2):
-                v = rho[g + 1, at_row(at, e), :]
-                mid[g + 1, at_row(at, e), :] = v * slope + stencil(rho, g, at, e, v)
-
-    def step_out(g):
-        vis = [planes_of(visitor_ref, j, g) for j in range(2)]
-        for i in range(2):
-            for e in range(2):
-                total = None
-                for at in range(4):
-                    if PAIRS[at][0] == i:
-                        v = mid[g + 1, at_row(at, e), :]
-                        pot = rho[g + 1, at_row(at, e), :] * base + stencil(mid, g, at, e, v)
-                        j = PAIRS[at][1]
-                        term = (weight[j] * vis[j][e]) * pot
-                        total = term if total is None else total + term
-                if running_ref is not None:
-                    total = total + running_ref[i, 8 * e : 8 * e + 8, columns(g)]
-                out_ref[i, 8 * e : 8 * e + 8, columns(g)] = total
+    def step_mid(n):
+        g0 = n * CHUNK
+        nb = stencils(rho, g0, CHUNK)
+        for (k, at, e), s in nb.items():
+            mid[g0 + k + 1, at_row(at, e), :] = rho[g0 + k + 1, at_row(at, e), :] * slope + s
+
+    def step_out(n):
+        g0 = n * CHUNK
+        nb = stencils(mid, g0, CHUNK)
+        for k in range(CHUNK):
+            g = g0 + k
+            vis = [planes_of(visitor_ref, j, g) for j in range(2)]
+            for i in range(2):
+                for e in range(2):
+                    total = None
+                    for at in range(4):
+                        if PAIRS[at][0] == i:
+                            pot = rho[g + 1, at_row(at, e), :] * base + nb[k, at, e]
+                            j = PAIRS[at][1]
+                            term = (weight[j] * vis[j][e]) * pot
+                            total = term if total is None else total + term
+                    if not first:
+                        total = total + running_ref[i, 8 * e : 8 * e + 8, columns(g)]
+                    out_ref[i, 8 * e : 8 * e + 8, columns(g)] = total
 
     sweep(step_rho, groups, UNROLL_RHO)
-    sweep(step_mid, groups, UNROLL_MID)
-    sweep(step_out, groups, UNROLL_OUT)
+    sweep(step_mid, groups // CHUNK, 1)
+    sweep(step_out, groups // CHUNK, 1)
 
 
 def edge_kernel(own_ref, own_halo_ref, *rest):
@@ -249,16 +282,18 @@
     )(orbitals, occupation)
 
 
-def visit(own, visitor, running):
+def visit(own, visitor, running=None, table=None):
     shape = (*own.shape[:2], own.shape[2] - LANES)
     groups = shape[2] // LANES
-    operands = [in_vmem(x) for x in (own, visitor) + (() if running is None else (running,))]
+    first = running is None
+    operands = [in_vmem(x) for x in (own, visitor) + (() if first else (running, table))]
     held = pltpu.VMEM((groups + 2, 104, LANES), jnp.float32)
+    out = pltpu.VMEM(shape, jnp.float32)
     return pl.pallas_call(
         visit_kernel,
-        out_shape=pltpu.VMEM(shape, jnp.float32),
+        out_shape=[out, pltpu.VMEM((2 * LANES, 2 * LANES), jnp.bfloat16)] if first else out,
         in_specs=[VMEM] * len(operands),
-        out_specs=VMEM,
+        out_specs=[VMEM] * 2 if first else VMEM,
         scratch_shapes=[held, held],
         name="visit",
     )(*operands)
@@ -309,10 +344,10 @@
     halo_two = from_two_back(halo)
     halo_other = across_pair_and_three(halo)
     halo_swapped = swapped_in_pair(halo_two)
-    running = visit(wide, wide, None)
-    running = visit(wide, two_back, running)
-    running = visit(wide, swapped, running)
-    running = visit(wide, other, running)
+    running, table = visit(wide, wide)
+    running = visit(wide, two_back, running, table)
+    running = visit(wide, swapped, running, table)
+    running = visit(wide, other, running, table)
     return finish(wide, halo, (wide, two_back, swapped, other), (halo, halo_two, halo_swapped, halo_other), running)
 
 

time: 46.1 us -> 39.7 us (0.86)
  waiting for transfers between devices: 15.9 us -> 9.75 us
  Pallas kernels: 11.8 us -> 8.74 us
  starting transfers between devices: 18.1 us -> 20.9 us
    ppermute x2, waiting for transfers between devices: 15.9 us -> 9.73 us  [from_two_back(): lax.ppermute(array, 'band', [(i, (i + 2) % size) for i in range(size)])]
    pallas_call x4, Pallas kernels: 8.49 us -> 5.44 us  [visit(): pl.pallas_call(visit_kernel, out_shape=[out, pltpu.VMEM((2 * LANES, 2 * L...]
    ppermute x2, starting transfers between devices: 2.86 us -> 5.89 us  [swapped_in_pair(): return lax.ppermute(array, 'band', [(i, i ^ 1) for i in range(size)])]
  transfers between devices with their start and end apart: 8 -> 8, of which waited for: 2 -> 2; matrix products, arithmetic and copies ran while one was open for 0% -> 0% of each run, Pallas kernels for 18% -> 14%
where the time goes in v3:
time: 39.7 us; the launch traced here: 39.6 us
  starting transfers between devices  20.9 us (53%)
  waiting for transfers between devices  9.75 us (25%)
  Pallas kernels  8.74 us (22%)
    ppermute x2, waiting for transfers between devices, from_two_back(): lax.ppermute(array, 'band', [(i, (i + 2) % size) for i in range(size)])  9.73 us
    ppermute x2, starting transfers between devices, across_pair_and_three(): lax.ppermute(array, 'band', [(i, (i + 1 + 2 * (i % 2)) % size) for i in r...  6.58 us
    ppermute x1, starting transfers between devices, per_device(): lax.ppermute(first, 'slab', [(i, i ^ 1) for i in range(size)])  6.05 us
    ppermute x2, starting transfers between devices, swapped_in_pair(): return lax.ppermute(array, 'band', [(i, i ^ 1) for i in range(size)])  5.89 us
    pallas_call x4, Pallas kernels, visit(): pl.pallas_call(visit_kernel, out_shape=[out, pltpu.VMEM((2 * LANES, 2 * L...  5.44 us
    pallas_call x1, Pallas kernels, finish(): pl.pallas_call(edge_kernel, out_shape=jax.ShapeDtypeStruct(running.shape,...  2.2 us
    ppermute x2, starting transfers between devices, from_two_back(): lax.ppermute(array, 'band', [(i, (i + 2) % size) for i in range(size)])  1.72 us
    pallas_call x1, Pallas kernels, prepare(): pl.pallas_call(lambda *refs: prepare_kernel(*refs, even_of=even_of), out_...  1.1 us
  transfers between devices with their start and end apart: 8, of which 2 were waited for; matrix products, arithmetic and copies ran while one was open for 0% of the time, Pallas kernels for 14%

profile of v3, /device:TPU:1, one launch (start us, length us, event | category | flops | bytes accessed | tf_op | source)
XLA Modules:
  0.0 39.6 jit_solution(7670363864681275169)
XLA Ops:
  0.0 1.1 %prepare.1 = (bf16[2,16,4224]{2,1,0:T(8,128)(2,1)S(1)}, bf16[4,4224]{1,0:T(4,128)(2,1)S(1)}, bf16[4,4224]{1,0:T(4,128)(2,1)S(1)}) custom-call(bf16[2,16,4096]{2,1,0:T(8,128)(2,1)} %refs_0_.1, bf16[2]{0:T(256)(128)(2,1)} %refs_1_.1), custom_call_target="tpu_custom_call" | custom-call | tf_op jit(solution)/shard_map/prepare/pallas_call | solution.py:272
  1.1 0.7 %collective-permute-start = (bf16[4,4224]{1,0:T(4,128)(2,1)S(1)}, bf16[4,4224]{1,0:T(4,128)(2,1)S(1)}, u32[]{:S(2)}, u32[]{:S(2)}) collective-permute-start(bf16[4,4224]{1,0:T(4,128)(2,1)S(1)} %get-tuple-element.11), channel_id=1, source_target_pairs={{1,2},{2,1},{3,4},{4,3},{5,6},{6,5},{9,10},{10,9},{11,12},{12,11},... | collective-permute-start | bytes 101384 | tf_op jit(solution)/shard_map/ppermute | solution.py:338
  1.8 6.0 %collective-permute-start.1 = (bf16[4,4224]{1,0:T(4,128)(2,1)S(1)}, bf16[4,4224]{1,0:T(4,128)(2,1)S(1)}, u32[]{:S(2)}, u32[]{:S(2)}) collective-permute-start(bf16[4,4224]{1,0:T(4,128)(2,1)S(1)} %get-tuple-element.12), channel_id=1, source_target_pairs={{0,1},{1,0},{2,3},{3,2},{4,5},{5,4},{6,7},{7,6},{8,9},{9,8},{10,11... | collective-permute-start | bytes 101384 | tf_op jit(solution)/shard_map/ppermute | solution.py:339
  7.8 1.6 %collective-permute-start.2 = (bf16[2,16,4224]{2,1,0:T(8,128)(2,1)S(1)}, bf16[2,16,4224]{2,1,0:T(8,128)(2,1)S(1)}, u32[]{:S(2)}, u32[]{:S(2)}) collective-permute-start(bf16[2,16,4224]{2,1,0:T(8,128)(2,1)S(1)} %get-tuple-element.10.refs_0_.refs_1_.own_ref.rest_0_), channel_id=1, source_target_pairs={{0,16},{8,24},{16,32},{24,40},{32,48},{40,56},{48,64},{56,72},{64,... | collective-permute-start | bytes 811016 | tf_op jit(solution)/shard_map/ppermute | solution.py:321
  9.5 4.4 %collective-permute-start.4 = (bf16[2,16,4224]{2,1,0:T(8,128)(2,1)S(1)}, bf16[2,16,4224]{2,1,0:T(8,128)(2,1)S(1)}, u32[]{:S(2)}, u32[]{:S(2)}) collective-permute-start(bf16[2,16,4224]{2,1,0:T(8,128)(2,1)S(1)} %get-tuple-element.10.refs_0_.refs_1_.own_ref.rest_0_), channel_id=1, source_target_pairs={{0,8},{8,32},{16,24},{24,48},{32,40},{40,64},{48,56},{56,80},{64,7... | collective-permute-start | bytes 811016 | tf_op jit(solution)/shard_map/ppermute | solution.py:326
  13.9 0.0 collective-permute-done
  13.9 0.0 collective-permute-done.1
  13.9 6.1 %collective-permute-done.2.refs_1_.rest_1_ = bf16[2,16,4224]{2,1,0:T(8,128)(2,1)S(1)} collective-permute-done((bf16[2,16,4224]{2,1,0:T(8,128)(2,1)S(1)}, bf16[2,16,4224]{2,1,0:T(8,128)(2,1)S(1)}, u32[]{:S(2)}, u32[]{:S(2)}) %collective-permute-start.2) | collective-permute-done | bytes 270368 | tf_op jit(solution)/shard_map/ppermute | solution.py:321
  20.0 4.4 %collective-permute-start.3 = (bf16[2,16,4224]{2,1,0:T(8,128)(2,1)S(1)}, bf16[2,16,4224]{2,1,0:T(8,128)(2,1)S(1)}, u32[]{:S(2)}, u32[]{:S(2)}) collective-permute-start(bf16[2,16,4224]{2,1,0:T(8,128)(2,1)S(1)} %collective-permute-done.2.refs_1_.rest_1_), channel_id=1, source_target_pairs={{0,8},{8,0},{16,24},{24,16},{32,40},{40,32},{48,56},{56,48},{64,72... | collective-permute-start | bytes 811016 | tf_op jit(solution)/shard_map/ppermute | solution.py:331
  24.4 0.1 collective-permute-start.5
  24.5 2.2 %collective-permute-start.7 = (bf16[8,4224]{1,0:T(8,128)(2,1)S(1)}, bf16[8,4224]{1,0:T(8,128)(2,1)S(1)}, u32[]{:S(2)}, u32[]{:S(2)}) collective-permute-start(bf16[8,4224]{1,0:T(8,128)(2,1)S(1)} %pad_maximum_fusion.own_halo_ref.rest_4_), channel_id=1, source_target_pairs={{0,8},{8,32},{16,24},{24,48},{32,40},{40,64},{48,56},{56,80},{64,7... | collective-permute-start | bytes 202760 | tf_op jit(solution)/shard_map/ppermute | solution.py:326
  26.7 3.6 %collective-permute-done.5.rest_5_ = bf16[8,4224]{1,0:T(8,128)(2,1)S(1)} collective-permute-done((bf16[8,4224]{1,0:T(8,128)(2,1)S(1)}, bf16[8,4224]{1,0:T(8,128)(2,1)S(1)}, u32[]{:S(2)}, u32[]{:S(2)}) %collective-permute-start.5) | collective-permute-done | bytes 67616 | tf_op jit(solution)/shard_map/ppermute | solution.py:321
  30.3 1.5 %collective-permute-start.6 = (bf16[8,4224]{1,0:T(8,128)(2,1)S(1)}, bf16[8,4224]{1,0:T(8,128)(2,1)S(1)}, u32[]{:S(2)}, u32[]{:S(2)}) collective-permute-start(bf16[8,4224]{1,0:T(8,128)(2,1)S(1)} %collective-permute-done.5.rest_5_), channel_id=1, source_target_pairs={{0,8},{8,0},{16,24},{24,16},{32,40},{40,32},{48,56},{56,48},{64,72... | collective-permute-start | bytes 202760 | tf_op jit(solution)/shard_map/ppermute | solution.py:331
  31.8 1.4 %visit.4 = (f32[2,16,4096]{2,1,0:T(8,128)S(1)}, bf16[256,256]{1,0:T(8,128)(2,1)S(1)}) custom-call(bf16[2,16,4224]{2,1,0:T(8,128)(2,1)S(1)} %get-tuple-element.10.refs_0_.refs_1_.own_ref.rest_0_, bf16[2,16,4224]{2,1,0:T(8,128)(2,1)S(1)} %get-tuple-element.10.refs_0_.refs_1_.own_ref.rest_0_), custom_call_target="tpu_custom_call" | custom-call | tf_op jit(solution)/shard_map/visit/pallas_call | solution.py:292
  33.2 1.4 %visit.5.refs_2_ = f32[2,16,4096]{2,1,0:T(8,128)S(1)} custom-call(bf16[2,16,4224]{2,1,0:T(8,128)(2,1)S(1)} %get-tuple-element.10.refs_0_.refs_1_.own_ref.rest_0_, bf16[2,16,4224]{2,1,0:T(8,128)(2,1)S(1)} %collective-permute-done.2.refs_1_.rest_1_, f32[2,16,4096]{2,1,0:T(8,128)S(1)} %get-tuple-element.13.refs_2_, bf16[256,256]{1,0:T(8,128)(2,1)S(1)} %get-tuple-element.14.refs_3_), custom_call_target="tpu_custom_call" | custom-call | tf_op jit(solution)/shard_map/visit/pallas_call | solution.py:292
  34.6 0.0 collective-permute-done.3.refs_1_.rest_2_
  34.6 0.0 copy-start
  34.6 1.4 %visit.6.refs_2_ = f32[2,16,4096]{2,1,0:T(8,128)S(1)} custom-call(bf16[2,16,4224]{2,1,0:T(8,128)(2,1)S(1)} %get-tuple-element.10.refs_0_.refs_1_.own_ref.rest_0_, bf16[2,16,4224]{2,1,0:T(8,128)(2,1)S(1)} %collective-permute-done.3.refs_1_.rest_2_, f32[2,16,4096]{2,1,0:T(8,128)S(1)} %visit.5.refs_2_, bf16[256,256]{1,0:T(8,128)(2,1)S(1)} %get-tuple-element.14.refs_3_), custom_call_target="tpu_custom_call" | custom-call | tf_op jit(solution)/shard_map/visit/pallas_call | solution.py:292
  35.9 0.0 copy-done
  36.0 0.0 collective-permute-done.4.refs_1_.rest_3_
  36.0 0.0 copy-start.1
  36.0 1.4 %visit.7.rest_8_ = f32[2,16,4096]{2,1,0:T(8,128)S(1)} custom-call(bf16[2,16,4224]{2,1,0:T(8,128)(2,1)S(1)} %get-tuple-element.10.refs_0_.refs_1_.own_ref.rest_0_, bf16[2,16,4224]{2,1,0:T(8,128)(2,1)S(1)} %collective-permute-done.4.refs_1_.rest_3_, f32[2,16,4096]{2,1,0:T(8,128)S(1)} %visit.6.refs_2_, bf16[256,256]{1,0:T(8,128)(2,1)S(1)} %get-tuple-element.14.refs_3_), custom_call_target="tpu_custom_call" | custom-call | tf_op jit(solution)/shard_map/visit/pallas_call | solution.py:292
  37.4 0.0 collective-permute-done.7.rest_7_
  37.4 0.0 collective-permute-done.6.rest_6_
  37.4 0.0 copy-done.1
  37.4 2.2 %finish.1 = f32[2,16,4096]{2,1,0:T(8,128)} custom-call(bf16[2,16,4224]{2,1,0:T(8,128)(2,1)S(1)} %get-tuple-element.10.refs_0_.refs_1_.own_ref.rest_0_, bf16[8,4224]{1,0:T(8,128)(2,1)S(1)} %pad_maximum_fusion.own_halo_ref.rest_4_, bf16[2,16,4224]{2,1,0:T(8,128)(2,1)S(1)} %get-tuple-element.10.refs_0_.refs_1_.own_ref.rest_0_, ...), custom_call_target="tpu_custom_call" | custom-call | tf_op jit(solution)/shard_map/finish/pallas_call | solution.py:306
  (2 shorter events, 0.1 us)
Async XLA Ops:
  1.1 12.8 %collective-permute-start = (bf16[4,4224]{1,0:T(4,128)(2,1)S(1)}, bf16[4,4224]{1,0:T(4,128)(2,1)S(1)}, u32[]{:S(2)}, u32[]{:S(2)}) collective-permute-start(bf16[4,4224]{1,0:T(4,128)(2,1)S(1)} %get-tuple-element.11), channel_id=1, source_target_pairs={{1,2},{2,1},{3,4},{4,3},{5,6},{6,5},{9,10},{10,9},{11,12},{12,11},... | collective-permute-start | bytes 101384 | tf_op jit(solution)/shard_map/ppermute | solution.py:338
  1.8 12.1 %collective-permute-start.1 = (bf16[4,4224]{1,0:T(4,128)(2,1)S(1)}, bf16[4,4224]{1,0:T(4,128)(2,1)S(1)}, u32[]{:S(2)}, u32[]{:S(2)}) collective-permute-start(bf16[4,4224]{1,0:T(4,128)(2,1)S(1)} %get-tuple-element.12), channel_id=1, source_target_pairs={{0,1},{1,0},{2,3},{3,2},{4,5},{5,4},{6,7},{7,6},{8,9},{9,8},{10,11... | collective-permute-start | bytes 101384 | tf_op jit(solution)/shard_map/ppermute | solution.py:339
  7.8 12.2 %collective-permute-start.2 = (bf16[2,16,4224]{2,1,0:T(8,128)(2,1)S(1)}, bf16[2,16,4224]{2,1,0:T(8,128)(2,1)S(1)}, u32[]{:S(2)}, u32[]{:S(2)}) collective-permute-start(bf16[2,16,4224]{2,1,0:T(8,128)(2,1)S(1)} %get-tuple-element.10.refs_0_.refs_1_.own_ref.rest_0_), channel_id=1, source_target_pairs={{0,16},{8,24},{16,32},{24,40},{32,48},{40,56},{48,64},{56,72},{64,... | collective-permute-start | bytes 811016 | tf_op jit(solution)/shard_map/ppermute | solution.py:321
  9.5 26.5 %collective-permute-start.4 = (bf16[2,16,4224]{2,1,0:T(8,128)(2,1)S(1)}, bf16[2,16,4224]{2,1,0:T(8,128)(2,1)S(1)}, u32[]{:S(2)}, u32[]{:S(2)}) collective-permute-start(bf16[2,16,4224]{2,1,0:T(8,128)(2,1)S(1)} %get-tuple-element.10.refs_0_.refs_1_.own_ref.rest_0_), channel_id=1, source_target_pairs={{0,8},{8,32},{16,24},{24,48},{32,40},{40,64},{48,56},{56,80},{64,7... | collective-permute-start | bytes 811016 | tf_op jit(solution)/shard_map/ppermute | solution.py:326
  20.0 14.5 %collective-permute-start.3 = (bf16[2,16,4224]{2,1,0:T(8,128)(2,1)S(1)}, bf16[2,16,4224]{2,1,0:T(8,128)(2,1)S(1)}, u32[]{:S(2)}, u32[]{:S(2)}) collective-permute-start(bf16[2,16,4224]{2,1,0:T(8,128)(2,1)S(1)} %collective-permute-done.2.refs_1_.rest_1_), channel_id=1, source_target_pairs={{0,8},{8,0},{16,24},{24,16},{32,40},{40,32},{48,56},{56,48},{64,72... | collective-permute-start | bytes 811016 | tf_op jit(solution)/shard_map/ppermute | solution.py:331
  24.4 5.9 %collective-permute-start.5 = (bf16[8,4224]{1,0:T(8,128)(2,1)S(1)}, bf16[8,4224]{1,0:T(8,128)(2,1)S(1)}, u32[]{:S(2)}, u32[]{:S(2)}) collective-permute-start(bf16[8,4224]{1,0:T(8,128)(2,1)S(1)} %pad_maximum_fusion.own_halo_ref.rest_4_), channel_id=1, source_target_pairs={{0,16},{8,24},{16,32},{24,40},{32,48},{40,56},{48,64},{56,72},{64,... | collective-permute-start | bytes 202760 | tf_op jit(solution)/shard_map/ppermute | solution.py:321
  24.5 12.8 %collective-permute-start.7 = (bf16[8,4224]{1,0:T(8,128)(2,1)S(1)}, bf16[8,4224]{1,0:T(8,128)(2,1)S(1)}, u32[]{:S(2)}, u32[]{:S(2)}) collective-permute-start(bf16[8,4224]{1,0:T(8,128)(2,1)S(1)} %pad_maximum_fusion.own_halo_ref.rest_4_), channel_id=1, source_target_pairs={{0,8},{8,32},{16,24},{24,48},{32,40},{40,64},{48,56},{56,80},{64,7... | collective-permute-start | bytes 202760 | tf_op jit(solution)/shard_map/ppermute | solution.py:326
  30.3 7.1 %collective-permute-start.6 = (bf16[8,4224]{1,0:T(8,128)(2,1)S(1)}, bf16[8,4224]{1,0:T(8,128)(2,1)S(1)}, u32[]{:S(2)}, u32[]{:S(2)}) collective-permute-start(bf16[8,4224]{1,0:T(8,128)(2,1)S(1)} %collective-permute-done.5.rest_5_), channel_id=1, source_target_pairs={{0,8},{8,0},{16,24},{24,16},{32,40},{40,32},{48,56},{56,48},{64,72... | collective-permute-start | bytes 202760 | tf_op jit(solution)/shard_map/ppermute | solution.py:331
  34.6 1.4 %copy-start = (bf16[2,16,4224]{2,1,0:T(8,128)(2,1)}, bf16[2,16,4224]{2,1,0:T(8,128)(2,1)S(1)}, u32[]{:S(2)}) copy-start(bf16[2,16,4224]{2,1,0:T(8,128)(2,1)S(1)} %collective-permute-done.3.refs_1_.rest_2_) | copy-start | bytes 811012
  36.0 1.4 %copy-start.1 = (bf16[2,16,4224]{2,1,0:T(8,128)(2,1)S(1)}, bf16[2,16,4224]{2,1,0:T(8,128)(2,1)}, u32[]{:S(2)}) copy-start(bf16[2,16,4224]{2,1,0:T(8,128)(2,1)} %copy-done) | copy-start | bytes 811012
